TPU v7x, 32 devices: a whole 2x2x4 slice. The times are simulated.
32 devices in a mesh: gz: 4 (over y, core), gy: 2 (over x), gx: 4 (over z).
Axes of the slice: x: 2, y: 2, z: 4, core: 2. Of those that a mesh axis runs over, the one named last changes fastest.
Arguments:
- positions: float32 [3, 4, 4, 32, 128], P(None, 'gx', 'gy', 'gz'), may hold values from 0 to 1
- counts: int32 [4, 4, 32], P('gx', 'gy', 'gz'), may hold values from 104 to 128
Outputs:
- energy: float32 [4, 4, 32, 128], P('gx', 'gy', 'gz')
- forces: float32 [3, 4, 4, 32, 128], P(None, 'gx', 'gy', 'gz')
Inputs may be any that keep to these rules, and one draw needn't show every extreme that they name: `counts`: slot k of a cell holds an atom exactly when k < its count; positions of other slots are not used.
All inputs are finite; a program needn't handle non-finite values.
Results may differ from a plain program's by a relative error of at most 0.0003.
Values sent between devices are 32-bit elements; how exact they have to be, the bound alone decides.
A program may use at most 64 MiB of HBM per device.

v0:
```python
import functools

import jax
import jax.numpy as jnp
from jax import lax
from jax.experimental import pallas as pl
from jax.experimental.pallas import tpu as pltpu
from jax.sharding import PartitionSpec as P

SENTINEL = 4.0
PAIR_SCALE = 0.02
EMBED_SCALE = 0.2
CUTOFF_SQUARED = 0.25
FORCE_SCALE = 8.0
FAR = -1.0e6
ROWS = 8


def split(value):
    first = value.astype(jnp.bfloat16).astype(jnp.float32)
    rest = value - first
    second = rest.astype(jnp.bfloat16).astype(jnp.float32)
    return first, second, rest - second


def far_rows(tile):
    b1, b2, b3 = split(tile)
    return jnp.concatenate([b1, b2, b1, b2, b3, b1], axis=0)


def own_rows(tile):
    a1, a2, a3 = split(tile)
    return jnp.concatenate([a1, a1, a2, a2, a1, a3], axis=0)


def place(index, sizes):
    return index // (sizes[1] * sizes[2]), index // sizes[2] % sizes[1], index % sizes[2]


def groups(sizes):
    depth = 2 if sizes[2] % 2 == 0 else 1
    plan = []
    for dx in range(3):
        for jy in range(sizes[1] + 2):
            for jz in range(depth + 2):
                ys = [y for y in range(sizes[1]) if 0 <= jy - y <= 2]
                zs = [z for z in range(depth) if 0 <= jz - z <= 2]
                if len(ys) == sizes[1]:
                    runs = [(True, [(y, z) for z in zs for y in ys])]
                else:
                    runs = [(False, [(y, z) for z in zs]) for y in ys]
                plan.append((dx, jy, jz, runs))
    return depth, plan


def side_by_side(tiles, sizes, depth, layer_first):
    order = (
        [(y, z) for z in range(depth) for y in range(sizes[1])]
        if layer_first
        else [(y, z) for y in range(sizes[1]) for z in range(depth)]
    )
    return {key: at for at, key in enumerate(order)}, jnp.concatenate(
        [tiles[key] for key in order], axis=1
    )


def far_tile(tile, index, wide):
    row = lax.broadcasted_iota(jnp.int32, tile.shape, 0)
    steps = [at.astype(jnp.float32) - 0.5 * size for at, size in zip(index, wide)]
    shift = jnp.where(row == 0, steps[0], jnp.where(row == 1, steps[1], steps[2]))
    filled = tile[0:1] < 2.0
    coords = jnp.where(filled & (row < 3), tile + shift, 0.0)
    near = -4.0 * jnp.sum(coords * coords, axis=0, keepdims=True)
    upper = jnp.where(row == 3, jnp.where(filled, near, FAR), coords)
    lower = jnp.where(row == 0, 1.0, 0.0)
    return jnp.concatenate([upper, lower], axis=0)


def own_tile(tile, index, wide):
    row = lax.broadcasted_iota(jnp.int32, tile.shape, 0)
    far = far_tile(tile, index, wide)
    coords = jnp.where(row < 3, far[:4], 0.0)
    near = 4.0 * jnp.sum(coords * coords, axis=0, keepdims=True)
    upper = jnp.where(row == 3, 1.0, 8.0 * coords)
    lower = jnp.where(row == 0, 1.0 - near, 0.0)
    return jnp.concatenate([upper, lower], axis=0)


NAMES = ("gx", "gy", "gz")
DIRECTIONS = [
    (x, y, z) for x in (-1, 0, 1) for y in (-1, 0, 1) for z in (-1, 0, 1) if (x, y, z) != (0, 0, 0)
]
DIRECTIONS.sort(key=lambda step: -sum(abs(o) for o in step))


def device_at(counts, step):
    return {
        name: lax.rem(lax.axis_index(name) + (offset + count), count)
        for name, offset, count in zip(NAMES, step, counts)
    }


def meet(counts):
    barrier = pltpu.get_barrier_semaphore()
    partners = sorted({tuple(o % c for o, c in zip(step, counts)) for step in DIRECTIONS})
    for step in partners:
        pl.semaphore_signal(
            barrier,
            inc=1,
            device_id=device_at(counts, step),
            device_id_type=pl.DeviceIdType.MESH,
        )
    pl.semaphore_wait(barrier, len(partners))


def send_rims(counts, source, target, sent, landed):
    sizes = source.shape[:3]
    copies = []
    for at, step in enumerate(DIRECTIONS):
        here = tuple(
            pl.ds(0, size) if o == 0 else pl.ds(size - 1 if o > 0 else 0, 1)
            for o, size in zip(step, sizes)
        )
        there = tuple(
            pl.ds(1, size) if o == 0 else pl.ds(0 if o > 0 else size + 1, 1)
            for o, size in zip(step, sizes)
        )
        copy = pltpu.make_async_remote_copy(
            src_ref=source.at[here],
            dst_ref=target.at[there],
            send_sem=sent.at[at],
            recv_sem=landed.at[at],
            device_id=device_at(counts, step),
            device_id_type=pl.DeviceIdType.MESH,
        )
        copy.start()
        copies.append(copy)
    return copies


def drain(copies, sizes, column_work):
    def arrive(chosen):
        for step, copy in zip(DIRECTIONS, copies):
            if chosen(step):
                copy.wait()

    arrive(lambda step: step[:2] == (0, 0))
    column_work(sizes[0] * sizes[1], lambda i: (i // sizes[1] + 1, i % sizes[1] + 1))
    arrive(lambda step: step[0] == 0 and step[1] != 0)
    column_work(2 * sizes[0], lambda i: (i // 2 + 1, i % 2 * (sizes[1] + 1)))
    arrive(lambda step: step[0] != 0 and step[1] == 0)
    column_work(2 * sizes[1], lambda i: (i % 2 * (sizes[0] + 1), i // 2 + 1))
    arrive(lambda step: step[0] != 0 and step[1] != 0)
    column_work(4, lambda i: (i % 2 * (sizes[0] + 1), i // 2 * (sizes[1] + 1)))


def kernel(
    counts,
    source,
    energy_ref,
    force_ref,
    ext,
    gain_own,
    gain_ext,
    turned,
    flat,
    column,
    sent,
    landed,
    gain_sent,
    gain_landed,
):
    sizes = source.shape[:3]
    wide = ext.shape[:3]
    slots = source.shape[-1]
    depth, plan = groups(sizes)
    keys = [(y, z) for y in range(sizes[1]) for z in range(depth)]
    steps = sizes[2] // depth

    meet(counts)
    copies = send_rims(counts, source, ext, sent, landed)

    inner = tuple(slice(1, 1 + size) for size in sizes)
    ext[inner] = source[...]

    def prepare(x, y):
        for z in range(wide[2]):
            b1, b2, b3 = split(far_tile(ext[x, y, z], (x, y, jnp.int32(z)), wide))
            across = jnp.concatenate([b1, b2, b1, b2, b3, b1], axis=0).T
            turned[x, y, z] = across.astype(jnp.bfloat16)
            rows = jnp.concatenate([b1, b2, b3, jnp.zeros_like(b1)], axis=0).astype(jnp.bfloat16)
            flat[x, y, z] = jnp.concatenate([rows, rows], axis=1)

    def looped(body):
        def work(count, where):
            def step(index, carry):
                body(*where(index))
                return carry

            lax.fori_loop(0, count, step, 0)

        return work

    drain(copies, sizes, looped(prepare))

    def group_tiles(x, z0):
        return {
            (y, z): own_tile(ext[x + 1, y + 1, z0 + z + 1], (x + 1, jnp.int32(y + 1), z0 + z + 1), wide)
            for y, z in keys
        }

    def group_packs(tiles):
        rows = {key: own_rows(tile).astype(jnp.bfloat16) for key, tile in tiles.items()}
        return {flag: side_by_side(rows, sizes, depth, flag) for flag in (True, False)}

    def density_group(index, carry):
        x, z0 = index // steps, index % steps * depth
        packs = group_packs(group_tiles(x, z0))
        rho = {key: jnp.zeros((ROWS, slots), jnp.float32) for key in keys}
        quartic = {key: jnp.zeros((ROWS, slots), jnp.float32) for key in keys}
        for dx, jy, jz, runs in plan:
            rows = turned[x + dx, jy, z0 + jz]
            for flag, targets in runs:
                order, pack = packs[flag]
                start = order[targets[0]] * slots
                pack = pack[:, start : start + len(targets) * slots]
                both = jnp.dot(rows, pack, preferred_element_type=jnp.float32)
                for at, key in enumerate(targets):
                    w = jnp.maximum(both[:, at * slots : (at + 1) * slots], 0.0)
                    s = w * w
                    q = s * s
                    rho[key] = rho[key] + jnp.sum(s.reshape(-1, ROWS, slots), axis=0)
                    quartic[key] = quartic[key] + jnp.sum(q.reshape(-1, ROWS, slots), axis=0)
        for y, z in keys:
            filled = ext[x + 1, y + 1, z0 + z + 1][0:1] < 2.0
            first = jnp.sum(rho[y, z], axis=0, keepdims=True) - 1.0
            second = jnp.sum(quartic[y, z], axis=0, keepdims=True) - 1.0
            first = jnp.where(filled, first, 0.0)
            pair_sum = PAIR_SCALE * (second - 2.0 * first)
            energy = -EMBED_SCALE * jnp.sqrt(first + 1.0) + 0.5 * pair_sum
            energy_ref[x, y, pl.ds(z0 + z, 1)] = jnp.where(filled, energy, 0.0)
            fprime = -0.5 * EMBED_SCALE * lax.rsqrt(first + 1.0)
            gain = 0.5 - fprime * (0.5 / PAIR_SCALE)
            gain_own[x, y, z0 + z] = gain
            gain_ext[x + 1, y + 1, z0 + z + 1] = gain
        return carry

    lax.fori_loop(0, sizes[0] * steps, density_group, 0)
    copies = send_rims(counts, gain_own, gain_ext, gain_sent, gain_landed)

    def raise_gain(x, y):
        rows = [gain_ext[x, y, z] for z in range(wide[2])]
        rows += [jnp.zeros((1, slots), jnp.float32)] * (-wide[2] % ROWS)
        column[x, y, :, : len(rows)] = jnp.concatenate(rows, axis=0).T

    drain(copies, sizes, looped(raise_gain))

    def force_group(index, carry):
        x, z0 = index // steps, index % steps * depth
        tiles = group_tiles(x, z0)
        packs = group_packs(tiles)
        gains = {(y, z): gain_own[x, y, z0 + z] for y, z in keys}
        total = {key: jnp.zeros((4 * ROWS, slots), jnp.float32) for key in keys}
        for dx, jy, jz, runs in plan:
            rows = turned[x + dx, jy, z0 + jz]
            moments = flat[x + dx, jy, z0 + jz]
            if jz == 0:
                lanes = pltpu.roll(column[x + dx, jy], slots - z0, 1)
            far_gain = jnp.broadcast_to(lanes[:, jz : jz + 1], (slots, slots))
            for flag, targets in runs:
                order, pack = packs[flag]
                start = order[targets[0]] * slots
                pack = pack[:, start : start + len(targets) * slots]
                both = jnp.dot(rows, pack, preferred_element_type=jnp.float32)
                highs, lows = [], []
                for at, key in enumerate(targets):
                    w = jnp.maximum(both[:, at * slots : (at + 1) * slots], 0.0)
                    f = w * ((far_gain + gains[key]) - w * w)
                    high = f.astype(jnp.bfloat16)
                    highs.append(high)
                    lows.append((f - high.astype(jnp.float32)).astype(jnp.bfloat16))
                stacked = jnp.concatenate(
                    [jnp.concatenate(highs, axis=1), jnp.concatenate(lows, axis=1)], axis=0
                )
                part = jnp.dot(moments, stacked, preferred_element_type=jnp.float32)
                for at, key in enumerate(targets):
                    total[key] = total[key] + part[:, at * slots : (at + 1) * slots]
        scale = FORCE_SCALE * 4.0 * PAIR_SCALE
        for y, z in keys:
            parts = total[y, z]
            whole = parts[:ROWS] + parts[ROWS : 2 * ROWS] + parts[2 * ROWS : 3 * ROWS]
            filled = ext[x + 1, y + 1, z0 + z + 1][0:1] < 2.0
            push = scale * (whole - 0.125 * tiles[y, z] * whole[4:5])
            push = jnp.where(filled, push, 0.0)
            for component in range(3):
                force_ref[component, x, y, pl.ds(z0 + z, 1)] = push[component : component + 1]
        return carry

    lax.fori_loop(0, sizes[0] * steps, force_group, 0)


def per_device(mesh_counts, positions, counts):
    slots = positions.shape[-1]
    sizes = positions.shape[1:4]
    wide = tuple(size + 2 for size in sizes)
    occupied = jnp.arange(slots, dtype=jnp.int32) < counts[..., None]
    seated = jnp.where(occupied[None], positions, SENTINEL)
    source = jnp.stack([seated[0], seated[1], seated[2], jnp.zeros_like(seated[0])], axis=3)
    return pl.pallas_call(
        functools.partial(kernel, mesh_counts),
        out_shape=(
            jax.ShapeDtypeStruct(sizes + (slots,), jnp.float32),
            jax.ShapeDtypeStruct((3,) + sizes + (slots,), jnp.float32),
        ),
        in_specs=[pl.BlockSpec(memory_space=pltpu.VMEM)],
        out_specs=(pl.BlockSpec(memory_space=pltpu.VMEM),) * 2,
        scratch_shapes=[
            pltpu.VMEM(wide + (4, slots), jnp.float32),
            pltpu.VMEM(sizes + (1, slots), jnp.float32),
            pltpu.VMEM(wide + (1, slots), jnp.float32),
            pltpu.VMEM(wide + (slots, 6 * ROWS), jnp.bfloat16),
            pltpu.VMEM(wide + (4 * ROWS, 2 * slots), jnp.bfloat16),
            pltpu.VMEM(wide[:2] + (slots, slots), jnp.float32),
        ]
        + [pltpu.SemaphoreType.DMA((len(DIRECTIONS),))] * 4,
        compiler_params=pltpu.CompilerParams(collective_id=0, has_side_effects=True),
        name="atoms",
    )(source)


def solution(mesh):
    placed = (P(None, "gx", "gy", "gz", None), P("gx", "gy", "gz"))
    return jax.shard_map(
        functools.partial(per_device, tuple(mesh.shape[name] for name in NAMES)),
        mesh=mesh,
        in_specs=placed,
        out_specs=(P("gx", "gy", "gz", None), P(None, "gx", "gy", "gz", None)),
        check_vma=False,
    )
```

profile of v0, /device:TPU:0, one launch (start us, length us, event | category | flops | bytes accessed | tf_op | source)
XLA Modules:
  0.0 47.5 jit_solution(4878795921651592997)
XLA Ops:
  0.6 0.0 copy-start
  0.6 0.1 pad.3.clone
  0.7 0.6 %copy-done = s32[1,2,8]{2,1,0:T(2,128)S(1)} copy-done((s32[1,2,8]{2,1,0:T(2,128)S(1)}, s32[1,2,8]{2,1,0:T(2,128)}, u32[]{:S(2)}) %copy-start) | copy-done | bytes 88
  1.3 0.1 iota_compare_fusion
  1.4 0.7 %broadcast_select_fusion = f32[3,1,2,8,128]{4,3,2,1,0:T(8,128)S(1)} fusion(f32[3,1,2,8,128]{4,3,2,1,0:T(8,128)} %param.2, pred[2,8,128]{2,1,0:T(8,128)(4,1)S(1)} %iota_compare_fusion), kind=kLoop, calls=%fused_computation.1 | loop fusion | flops 6144 | bytes 51200 | tf_op jit(solution)/shard_map/jit(_where)/select_n | solution.py:307
  2.1 0.7 %maximum_maximum_fusion.source = f32[1,2,8,4,128]{4,3,2,1,0:T(4,128)} fusion(f32[1,2,8,1,128]{4,3,2,1,0:T(1,128)S(1)} %bitcast.10, f32[1,2,8,1,128]{4,3,2,1,0:T(1,128)S(1)} %bitcast.11, f32[1,2,8,1,128]{4,3,2,1,0:T(1,128)S(1)} %bitcast.9, f32[4]{0:T(128)S(1)} %pad.3.clone), kind=kLoop, calls=%fused_computation | loop fusion | flops 24576 | bytes 57360 | tf_op jit(solution)/shard_map/stack | solution.py:308
  2.8 42.0 %atoms.1 = (f32[1,2,8,128]{3,2,1,0:T(8,128)}, f32[3,1,2,8,128]{4,3,2,1,0:T(8,128)}) custom-call(f32[1,2,8,4,128]{4,3,2,1,0:T(4,128)} %maximum_maximum_fusion.source), custom_call_target="tpu_custom_call" | custom-call | tf_op jit(solution)/shard_map/atoms/pallas_call | solution.py:309
  44.8 1.3 %copy.8 = f32[1,2,8,128]{3,2,1,0:T(8,128)} copy(f32[1,2,8,128]{3,2,1,0:T(8,128)} %get-tuple-element.7) | data formatting | bytes 16384
  46.1 1.3 %copy.9 = f32[3,1,2,8,128]{4,3,2,1,0:T(8,128)} copy(f32[3,1,2,8,128]{4,3,2,1,0:T(8,128)} %get-tuple-element.8) | data formatting | bytes 49152
  (1 shorter events, 0.0 us)
Async XLA Ops:
  0.6 0.7 %copy-start = (s32[1,2,8]{2,1,0:T(2,128)S(1)}, s32[1,2,8]{2,1,0:T(2,128)}, u32[]{:S(2)}) copy-start(s32[1,2,8]{2,1,0:T(2,128)} %param.3) | copy-start | bytes 196
where the time goes:
time: 47.8 us; the launch traced here: 47.5 us
  Pallas kernels  42 us (88%)
  local copies, waits for them, and re-layouts  3.32 us (7%)
  other arithmetic  1.5 us (3%)
  between operations  0.65 us (1%)
    pallas_call x1, Pallas kernels, per_device(): pl.pallas_call(functools.partial(kernel, mesh_counts), out_shape=(jax.Sha...  42 us
    unnamed x4, local copies, waits for them, and re-layouts  3.24 us

commit v1 on v0

v1 whole, which is shorter than its diff:
```python
import functools

import jax
import jax.numpy as jnp
from jax import lax
from jax.experimental import pallas as pl
from jax.experimental.pallas import tpu as pltpu
from jax.sharding import PartitionSpec as P

SENTINEL = 4.0
PAIR_SCALE = 0.02
EMBED_SCALE = 0.2
FORCE_SCALE = 8.0
FAR = -1.0e6
ROWS = 8
OCTANTS = 8
HALF = 64


def split(value):
    first = value.astype(jnp.bfloat16).astype(jnp.float32)
    rest = value - first
    second = rest.astype(jnp.bfloat16).astype(jnp.float32)
    return first, second, rest - second


NAMES = ("gx", "gy", "gz")
DIRECTIONS = [
    (x, y, z) for x in (-1, 0, 1) for y in (-1, 0, 1) for z in (-1, 0, 1) if (x, y, z) != (0, 0, 0)
]
DIRECTIONS.sort(key=lambda step: -sum(abs(o) for o in step))


def device_at(counts, step):
    return {
        name: lax.rem(lax.axis_index(name) + (offset + count), count)
        for name, offset, count in zip(NAMES, step, counts)
    }


def partners(counts):
    return sorted({tuple(o % c for o, c in zip(step, counts)) for step in DIRECTIONS})


def greet(counts):
    barrier = pltpu.get_barrier_semaphore()
    for step in partners(counts):
        pl.semaphore_signal(
            barrier,
            inc=1,
            device_id=device_at(counts, step),
            device_id_type=pl.DeviceIdType.MESH,
        )


def meet(counts):
    pl.semaphore_wait(pltpu.get_barrier_semaphore(), len(partners(counts)))


def send_rims(counts, source, target, sent, landed):
    sizes = source.shape[:3]
    copies = []
    for at, step in enumerate(DIRECTIONS):
        here = tuple(
            pl.ds(0, size) if o == 0 else pl.ds(size - 1 if o > 0 else 0, 1)
            for o, size in zip(step, sizes)
        )
        there = tuple(
            pl.ds(1, size) if o == 0 else pl.ds(0 if o > 0 else size + 1, 1)
            for o, size in zip(step, sizes)
        )
        copy = pltpu.make_async_remote_copy(
            src_ref=source.at[here],
            dst_ref=target.at[there],
            send_sem=sent.at[at],
            recv_sem=landed.at[at],
            device_id=device_at(counts, step),
            device_id_type=pl.DeviceIdType.MESH,
        )
        copy.start()
        copies.append(copy)
    return copies


def arrive(copies, chosen):
    for step, copy in zip(DIRECTIONS, copies):
        if chosen(step):
            copy.wait()


def own_plane(step):
    return step[0] == 0


def side_plane(step):
    return step[0] != 0


def kernel(
    mesh_counts,
    counts_ref,
    positions,
    energy_ref,
    force_ref,
    raw,
    source,
    ext,
    far,
    far_gain,
    gain_own,
    gain_ext,
    order,
    pieces_of,
    picks,
    weights,
    wide_rows,
    dense,
    gains,
    table_rows,
    table,
    raw_sem,
    table_sem,
    sent,
    landed,
    gain_sent,
    gain_landed,
):
    sizes = source.shape[:3]
    sx, sy, sz = sizes
    wide = ext.shape[:3]
    wx, wy, wz = wide
    slots = source.shape[-1]
    cells = sx * sy * sz
    group_count = weights.shape[1]
    depth = picks.shape[1]
    plane = wy * wz

    greet(mesh_counts)
    fetch = pltpu.make_async_copy(positions, raw, raw_sem)
    fetch.start()

    lane = lax.broadcasted_iota(jnp.int32, (cells, slots), 1)
    cell = lax.broadcasted_iota(jnp.int32, (cells, slots), 0)
    occupancy = jnp.zeros((cells, slots), jnp.int32)
    for x in range(sx):
        for y in range(sy):
            for z in range(sz):
                occupancy = jnp.where(cell == (x * sy + y) * sz + z, counts_ref[x, y, z], occupancy)
    filled = lane < occupancy
    column_of = sum(((cell >= k * sz).astype(jnp.int32) for k in range(1, sx * sy)), jnp.zeros_like(cell))
    plane_of = sum(((column_of >= k * sy).astype(jnp.int32) for k in range(1, sx)), jnp.zeros_like(cell))
    spots = (plane_of, column_of - plane_of * sy, cell - column_of * sz)

    fetch.wait()
    seated = [
        jnp.where(filled, raw[k].reshape(cells, slots), SENTINEL) for k in range(3)
    ]
    for k in range(3):
        source[:, :, :, k, :] = seated[k].reshape(sizes + (slots,))
    source[:, :, :, 3, :] = jnp.zeros(sizes + (slots,), jnp.float32)

    meet(mesh_counts)
    copies = send_rims(mesh_counts, source, ext, sent, landed)

    own = [
        jnp.where(
            filled,
            seated[k] + ((spots[k] + 1).astype(jnp.float32) - 0.5 * wide[k]),
            0.0,
        )
        for k in range(3)
    ]
    inner = tuple(slice(1, 1 + size) for size in sizes)
    ext[inner] = source[...]

    upper = [(seated[k] >= 0.5).astype(jnp.int32) for k in range(3)]
    octant = jnp.where(filled, 4 * upper[0] + 2 * upper[1] + upper[2], OCTANTS)
    members = jnp.concatenate(
        [jnp.where(octant == o, 1.0, 0.0) for o in range(OCTANTS)], axis=0
    ).astype(jnp.bfloat16)
    before = lax.broadcasted_iota(jnp.int32, (slots, 2 * slots), 0)
    after = lax.broadcasted_iota(jnp.int32, (slots, 2 * slots), 1)
    earlier = jnp.where((after >= slots) | (before < after), 1.0, 0.0).astype(jnp.bfloat16)
    ranks = jnp.dot(members, earlier, preferred_element_type=jnp.float32).astype(jnp.int32)
    start = jnp.zeros((cells, slots), jnp.int32)
    place = jnp.full((cells, slots), -1, jnp.int32)
    block = jnp.zeros((cells, slots), jnp.int32)
    group = jnp.where(lane >= HALF, lane - HALF, lane)
    for o in range(OCTANTS):
        rows = ranks[o * cells : (o + 1) * cells]
        place = jnp.where(octant == o, start + rows[:, :slots], place)
        if o:
            block = block + jnp.where(group * ROWS >= start, 1, 0)
        start = start + ((rows[:, slots:] + (ROWS - 1)) & -ROWS)
    order[...] = place
    corner = (
        ((spots[0] + 1) * wy + spots[1] + ((block >> 1) & 1)) * wz + spots[2] + (block & 1)
    )
    table_rows[...] = jnp.where(lane >= HALF, corner + (2 * (block >> 2) - 1) * plane, corner)
    tabulate = pltpu.make_async_copy(table_rows, table, table_sem)
    tabulate.start()

    near = 1.0 - 4.0 * (own[0] * own[0] + own[1] * own[1] + own[2] * own[2])
    for k, value in enumerate([8.0 * own[0], 8.0 * own[1], 8.0 * own[2], near]):
        for part, piece in enumerate(split(value)):
            pieces_of[part, k] = piece

    slot_lane = lax.broadcasted_iota(jnp.int32, (ROWS, slots), 1)

    def spread(column):
        return jnp.broadcast_to(column, (ROWS, slots))

    batch = next(n for n in (4, 2, 1) if cells % n == 0)

    def sort_cells(i, carry):
        found = []
        for j in range(batch):
            c = i * batch + j
            spot = order[pl.ds(c, 1), :]
            target = lax.broadcasted_iota(jnp.int32, (depth, slots), 0)
            pick = jnp.where(target == spot, 1.0, 0.0).astype(jnp.bfloat16)
            picks[c] = pick
            pieces = []
            for part in range(3):
                rows = [pieces_of[part, k, pl.ds(c, 1), :] for k in range(4)]
                pieces.append(jnp.concatenate(rows + [jnp.zeros((4, slots), jnp.float32)], axis=0))
            values = jnp.concatenate(pieces, axis=1).astype(jnp.bfloat16)
            found.append(
                lax.dot_general(
                    jnp.concatenate([pick, pick, pick], axis=1),
                    values,
                    (((1,), (1,)), ((), ())),
                    preferred_element_type=jnp.float32,
                )
            )
        for k in range(4):
            for j in range(batch):
                for g in range(group_count):
                    wide_rows[i * batch + j, g, k] = spread(
                        found[j][g * ROWS : (g + 1) * ROWS, k : k + 1]
                    )
        return carry

    lax.fori_loop(0, cells // batch, sort_cells, 0)

    def prepare(x, y):
        tile = ext[x, y]
        shape = (wz, ROWS, slots)
        rows = [jnp.broadcast_to(tile[:, k : k + 1, :], shape) for k in range(3)]
        there = rows[0] < 2.0
        floor = lax.broadcasted_iota(jnp.int32, shape, 0).astype(jnp.float32) - 0.5 * wz
        shifts = (
            lax.convert_element_type(x, jnp.float32) - 0.5 * wx,
            lax.convert_element_type(y, jnp.float32) - 0.5 * wy,
            floor,
        )
        coords = [jnp.where(there, row + shift, 0.0) for row, shift in zip(rows, shifts)]
        squares = coords[0] * coords[0] + coords[1] * coords[1] + coords[2] * coords[2]
        at = pl.ds((x * wy + y) * wz, wz)
        for k in range(3):
            far[at, k] = coords[k]
        far[at, 3] = jnp.where(there, -4.0 * squares, FAR)

    def prepare_gain(x, y):
        far_gain[pl.ds((x * wy + y) * wz, wz)] = jnp.broadcast_to(
            gain_ext[x, y], (wz, ROWS, slots)
        )

    def own_columns(body):
        def step(i, carry):
            body(i // wy + 1, i % wy)
            return carry

        lax.fori_loop(0, sx * wy, step, 0)

    def side_columns(body):
        def step(i, carry):
            body(i // wy * (wx - 1), i % wy)
            return carry

        lax.fori_loop(0, 2 * wy, step, 0)

    dense[...] = jnp.zeros_like(dense)

    def density(phase):
        def one_cell(c, carry):
            def one_group(g, inside):
                base = table[c, phase * HALF + g]
                xi, yi, zi, ci = (wide_rows[c, g, k] for k in range(4))
                if phase:
                    rho, quartic = wide_rows[c, g, 4], wide_rows[c, g, 5]
                else:
                    rho, quartic = (jnp.zeros((ROWS, slots), jnp.float32),) * 2
                for dy in range(2):
                    for dz in range(2):
                        at = base + (dy * wz + dz)
                        t = (far[at, 3] + ci) + xi * far[at, 0]
                        t = t + yi * far[at, 1] + zi * far[at, 2]
                        w = jnp.maximum(t, 0.0)
                        weights[c, g, 4 * phase + 2 * dy + dz] = w
                        s = w * w
                        rho = rho + s
                        quartic = quartic + s * s
                if phase:
                    first = jnp.sum(rho, axis=1, keepdims=True)
                    second = jnp.sum(quartic, axis=1, keepdims=True)
                    at = pl.ds(g * ROWS, ROWS)
                    dense[at, :] = jnp.where(
                        slot_lane == c,
                        first,
                        jnp.where(slot_lane == cells + c, second, dense[at, :]),
                    )
                else:
                    wide_rows[c, g, 4] = rho
                    wide_rows[c, g, 5] = quartic
                return inside

            lax.fori_loop(0, group_count, one_group, 0, unroll=True)
            return carry

        lax.fori_loop(0, cells, one_cell, 0)

    def unsort(value, kinds):
        turned = value.T[: kinds * cells, :depth]
        pieces = jnp.concatenate(split(turned), axis=0).astype(jnp.bfloat16)
        total = jnp.zeros((3 * kinds * cells, slots), jnp.float32)
        row = lax.broadcasted_iota(jnp.int32, pieces.shape, 0) % cells
        for c in range(cells):
            kept = jnp.where(row == c, pieces, jnp.zeros_like(pieces))
            total = total + jnp.dot(kept, picks[c], preferred_element_type=jnp.float32)
        size = kinds * cells
        return total[:size] + total[size : 2 * size] + total[2 * size :]

    arrive(copies, own_plane)
    own_columns(prepare)
    tabulate.wait()
    density(0)
    arrive(copies, side_plane)
    side_columns(prepare)
    density(1)

    first = jnp.maximum(dense[...] - 1.0, 0.0)
    second = pltpu.roll(first, slots - cells, 1)
    pair_sum = PAIR_SCALE * (second - 2.0 * first)
    energy = -EMBED_SCALE * jnp.sqrt(first + 1.0) + 0.5 * pair_sum
    fprime = -0.5 * EMBED_SCALE * lax.rsqrt(first + 1.0)
    gain = 0.5 - fprime * (0.5 / PAIR_SCALE)
    gains[...] = gain
    gain_rows = unsort(gain, 1)
    gain_own[...] = gain_rows.reshape(sizes + (1, slots))
    copies = send_rims(mesh_counts, gain_own, gain_ext, gain_sent, gain_landed)
    gain_ext[inner] = gain_rows.reshape(sizes + (1, slots))
    energy_rows = unsort(energy, 1)
    energy_ref[...] = jnp.where(filled, energy_rows, 0.0).reshape(sizes + (slots,))
    dense[...] = jnp.zeros_like(dense)

    def force(phase):
        def one_cell(c, carry):
            def one_group(g, inside):
                base = table[c, phase * HALF + g]
                rows = pl.ds(g * ROWS, ROWS)
                gi = wide_rows[c, g, 4]
                if phase:
                    parts = [wide_rows[c, g, k] for k in range(4)]
                else:
                    parts = [jnp.zeros((ROWS, slots), jnp.float32)] * 4
                for dy in range(2):
                    for dz in range(2):
                        at = base + (dy * wz + dz)
                        w = weights[c, g, 4 * phase + 2 * dy + dz]
                        f = w * ((far_gain[at] + gi) - w * w)
                        parts[0] = parts[0] + f
                        for k in range(3):
                            parts[k + 1] = parts[k + 1] + f * far[at, k]
                if phase:
                    kept = dense[rows, :]
                    for k in range(4):
                        kept = jnp.where(
                            slot_lane == k * cells + c,
                            jnp.sum(parts[k], axis=1, keepdims=True),
                            kept,
                        )
                    dense[rows, :] = kept
                else:
                    for k in range(4):
                        wide_rows[c, g, k] = parts[k]
                return inside

            lax.fori_loop(0, group_count, one_group, 0, unroll=True)
            return carry

        lax.fori_loop(0, cells, one_cell, 0)

    def spread_gains(g, carry):
        tile = gains[pl.ds(g * ROWS, ROWS), :]
        for c in range(cells):
            wide_rows[c, g, 4] = spread(tile[:, c : c + 1])
        return carry

    lax.fori_loop(0, group_count, spread_gains, 0)
    arrive(copies, own_plane)
    own_columns(prepare_gain)
    force(0)
    arrive(copies, side_plane)
    side_columns(prepare_gain)
    force(1)

    moments = unsort(dense[...], 4)
    scale = FORCE_SCALE * 4.0 * PAIR_SCALE
    for k in range(3):
        push = moments[(k + 1) * cells : (k + 2) * cells] - own[k] * moments[:cells]
        force_ref[k] = jnp.where(filled, scale * push, 0.0).reshape(sizes + (slots,))


def per_device(mesh_counts, positions, counts):
    slots = positions.shape[-1]
    sizes = positions.shape[1:4]
    wide = tuple(size + 2 for size in sizes)
    cells = sizes[0] * sizes[1] * sizes[2]
    far_cells = wide[0] * wide[1] * wide[2]
    groups = (slots + OCTANTS * (ROWS - 1)) // ROWS
    depth = -(-groups // 2) * 2 * ROWS
    tall = -(-depth // 128) * 128
    f32 = jnp.float32
    return pl.pallas_call(
        functools.partial(kernel, mesh_counts),
        out_shape=(
            jax.ShapeDtypeStruct(sizes + (slots,), f32),
            jax.ShapeDtypeStruct((3,) + sizes + (slots,), f32),
        ),
        in_specs=[
            pl.BlockSpec(memory_space=pltpu.SMEM),
            pl.BlockSpec(memory_space=pl.ANY),
        ],
        out_specs=(pl.BlockSpec(memory_space=pltpu.VMEM),) * 2,
        scratch_shapes=[
            pltpu.VMEM((3,) + sizes + (slots,), f32),
            pltpu.VMEM(sizes + (4, slots), f32),
            pltpu.VMEM(wide + (4, slots), f32),
            pltpu.VMEM((far_cells, 4, ROWS, slots), f32),
            pltpu.VMEM((far_cells, ROWS, slots), f32),
            pltpu.VMEM(sizes + (1, slots), f32),
            pltpu.VMEM(wide + (1, slots), f32),
            pltpu.VMEM((cells, slots), jnp.int32),
            pltpu.VMEM((3, 4, cells, slots), f32),
            pltpu.VMEM((cells, depth, slots), jnp.bfloat16),
            pltpu.VMEM((cells, groups, 8, ROWS, slots), f32),
            pltpu.VMEM((cells, groups, 6, ROWS, slots), f32),
            pltpu.VMEM((tall, slots), f32),
            pltpu.VMEM((tall, slots), f32),
            pltpu.VMEM((cells, slots), jnp.int32),
            pltpu.SMEM((cells, slots), jnp.int32),
            pltpu.SemaphoreType.DMA,
            pltpu.SemaphoreType.DMA,
        ]
        + [pltpu.SemaphoreType.DMA((len(DIRECTIONS),))] * 4,
        compiler_params=pltpu.CompilerParams(collective_id=0, has_side_effects=True),
        name="atoms",
    )(counts, positions)


def solution(mesh):
    placed = (P(None, "gx", "gy", "gz", None), P("gx", "gy", "gz"))
    return jax.shard_map(
        functools.partial(per_device, tuple(mesh.shape[name] for name in NAMES)),
        mesh=mesh,
        in_specs=placed,
        out_specs=(P("gx", "gy", "gz", None), P(None, "gx", "gy", "gz", None)),
        check_vma=False,
    )
```

time: 47.8 us -> 34.3 us (0.72)
  Pallas kernels: 42 us -> 30.7 us
  other arithmetic: 1.5 us -> 0 us
  local copies, waits for them, and re-layouts: 3.32 us -> 2.64 us
    pallas_call x1, Pallas kernels: 42 us -> 30.7 us  [per_device(): pl.pallas_call(functools.partial(kernel, mesh_counts), out_shape=(jax.Sha...]
    select_n x1 -> x0, other arithmetic: 0.74 us -> none  [per_device(): seated = jnp.where(occupied[None], positions, SENTINEL)]
    another operation x1 -> x0, other arithmetic: 0.69 us -> none  [per_device(): jnp.stack([seated[0], seated[1], seated[2], jnp.zeros_like(seated[0])], a...]
    unnamed x4 -> x2, local copies, waits for them, and re-layouts: 3.24 us -> 2.64 us
where the time goes in v1:
time: 34.3 us; the launch traced here: 34 us
  Pallas kernels  30.7 us (90%)
  local copies, waits for them, and re-layouts  2.64 us (8%)
  between operations  0.64 us (2%)
    pallas_call x1, Pallas kernels, per_device(): pl.pallas_call(functools.partial(kernel, mesh_counts), out_shape=(jax.Sha...  30.7 us
    unnamed x2, local copies, waits for them, and re-layouts  2.64 us

profile of v1, /device:TPU:0, one launch (start us, length us, event | category | flops | bytes accessed | tf_op | source)
XLA Modules:
  0.0 34.0 jit_solution(15629842747199944091)
XLA Ops:
  0.6 30.7 %atoms.1 = (f32[1,2,8,128]{3,2,1,0:T(8,128)}, f32[3,1,2,8,128]{4,3,2,1,0:T(8,128)}) custom-call(s32[1,2,8]{2,1,0:T(2,128)} %counts_ref.1, f32[3,1,2,8,128]{4,3,2,1,0:T(8,128)} %positions.1), custom_call_target="tpu_custom_call" | custom-call | tf_op jit(solution)/shard_map/atoms/pallas_call | solution.py:425
  31.4 1.3 %copy.6 = f32[1,2,8,128]{3,2,1,0:T(8,128)} copy(f32[1,2,8,128]{3,2,1,0:T(8,128)} %get-tuple-element.4) | data formatting | bytes 16384
  32.7 1.3 %copy.7 = f32[3,1,2,8,128]{4,3,2,1,0:T(8,128)} copy(f32[3,1,2,8,128]{4,3,2,1,0:T(8,128)} %get-tuple-element.5) | data formatting | bytes 49152

commit v2 on v1

v2 whole, which is shorter than its diff:
```python
import functools
import math

import jax
import jax.numpy as jnp
from jax import lax
from jax.experimental import pallas as pl
from jax.experimental.pallas import tpu as pltpu
from jax.sharding import PartitionSpec as P

SENTINEL = 4.0
PAIR_SCALE = 0.02
EMBED_SCALE = 0.2
FORCE_SCALE = 8.0
FAR = -1.0e6
ROWS = 8
OCTANTS = 8
SPAN = 32


def split(value):
    first = value.astype(jnp.bfloat16).astype(jnp.float32)
    rest = value - first
    second = rest.astype(jnp.bfloat16).astype(jnp.float32)
    return first, second, rest - second


NAMES = ("gx", "gy", "gz")
DIRECTIONS = [
    (x, y, z) for x in (-1, 0, 1) for y in (-1, 0, 1) for z in (-1, 0, 1) if (x, y, z) != (0, 0, 0)
]
DIRECTIONS.sort(key=lambda step: (abs(step[0]) * (1 + abs(step[1])), -sum(map(abs, step))))


def device_at(counts, step):
    return {
        name: lax.rem(lax.axis_index(name) + (offset + count), count)
        for name, offset, count in zip(NAMES, step, counts)
    }


def partners(counts):
    return sorted({tuple(o % c for o, c in zip(step, counts)) for step in DIRECTIONS})


def greet(counts):
    barrier = pltpu.get_barrier_semaphore()
    for step in partners(counts):
        pl.semaphore_signal(
            barrier,
            inc=1,
            device_id=device_at(counts, step),
            device_id_type=pl.DeviceIdType.MESH,
        )


def meet(counts):
    pl.semaphore_wait(pltpu.get_barrier_semaphore(), len(partners(counts)))


def send_rims(counts, source, target, sent, landed):
    lead = (slice(None),) * (source.ndim - 5)
    sizes = source.shape[-5:-2]
    copies = []
    for at, step in enumerate(DIRECTIONS):
        here = tuple(
            pl.ds(0, size) if o == 0 else pl.ds(size - 1 if o > 0 else 0, 1)
            for o, size in zip(step, sizes)
        )
        there = tuple(
            pl.ds(1, size) if o == 0 else pl.ds(0 if o > 0 else size + 1, 1)
            for o, size in zip(step, sizes)
        )
        copy = pltpu.make_async_remote_copy(
            src_ref=source.at[lead + here],
            dst_ref=target.at[lead + there],
            send_sem=sent.at[at],
            recv_sem=landed.at[at],
            device_id=device_at(counts, step),
            device_id_type=pl.DeviceIdType.MESH,
        )
        copy.start()
        copies.append(copy)
    return copies


def arrive(copies, chosen):
    for step, copy in zip(DIRECTIONS, copies):
        if chosen(step):
            copy.wait()


def own_plane(step):
    return step[0] == 0


def side_faces(step):
    return step[0] != 0 and step[1] == 0


def side_edges(step):
    return step[0] != 0 and step[1] != 0


def halves(value):
    high = value.astype(jnp.bfloat16)
    return high, (value - high.astype(jnp.float32)).astype(jnp.bfloat16)


def kernel(
    mesh_counts,
    counts,
    positions,
    energy_ref,
    force_ref,
    held,
    raw,
    source,
    ext,
    far,
    far_gain,
    gain_own,
    gain_ext,
    order,
    pieces_of,
    picks,
    weights,
    lanes_of,
    dense,
    table_rows,
    table,
    fetch_sem,
    table_sem,
    sent,
    landed,
    gain_sent,
    gain_landed,
):
    sizes = gain_own.shape[:3]
    sx, sy, sz = sizes
    wide = gain_ext.shape[:3]
    wx, wy, wz = wide
    slots = source.shape[-1]
    cells = sx * sy * sz
    group_count = weights.shape[1]
    depth = picks.shape[1]
    plane = wy * wz

    fetches = [
        pltpu.make_async_copy(counts, held, fetch_sem.at[0]),
        pltpu.make_async_copy(positions, raw, fetch_sem.at[1]),
    ]
    for fetch in fetches:
        fetch.start()
    greet(mesh_counts)

    lane = lax.broadcasted_iota(jnp.int32, (cells, slots), 1)
    cell = lax.broadcasted_iota(jnp.int32, (cells, slots), 0)
    column_of = sum(((cell >= k * sz).astype(jnp.int32) for k in range(1, sx * sy)), jnp.zeros_like(cell))
    plane_of = sum(((column_of >= k * sy).astype(jnp.int32) for k in range(1, sx)), jnp.zeros_like(cell))
    spots = (plane_of, column_of - plane_of * sy, cell - column_of * sz)

    for fetch in fetches:
        fetch.wait()
    occupancy = jnp.zeros((cells, slots), jnp.int32)
    for x in range(sx):
        for y in range(sy):
            for z in range(sz):
                occupancy = jnp.where(cell == (x * sy + y) * sz + z, held[x, y, z], occupancy)
    filled = lane < occupancy
    seated = [
        jnp.where(filled, raw[k].reshape(cells, slots), SENTINEL) for k in range(3)
    ]
    for k in range(3):
        source[k] = seated[k].reshape(sizes + (1, slots))

    meet(mesh_counts)
    copies = send_rims(mesh_counts, source, ext, sent, landed)

    own = [
        jnp.where(
            filled,
            seated[k] + ((spots[k] + 1).astype(jnp.float32) - 0.5 * wide[k]),
            0.0,
        )
        for k in range(3)
    ]
    inner = tuple(slice(1, 1 + size) for size in sizes)
    for k in range(3):
        ext[(k,) + inner] = seated[k].reshape(sizes + (1, slots))

    upper = [(seated[k] >= 0.5).astype(jnp.int32) for k in range(3)]
    octant = jnp.where(filled, 4 * upper[0] + 2 * upper[1] + upper[2], OCTANTS)
    members = jnp.concatenate(
        [jnp.where(octant == o, 1.0, 0.0) for o in range(OCTANTS)], axis=0
    ).astype(jnp.bfloat16)
    before = lax.broadcasted_iota(jnp.int32, (slots, 2 * slots), 0)
    after = lax.broadcasted_iota(jnp.int32, (slots, 2 * slots), 1)
    earlier = jnp.where((after >= slots) | (before < after), 1.0, 0.0).astype(jnp.bfloat16)
    ranks = jnp.dot(members, earlier, preferred_element_type=jnp.float32).astype(jnp.int32)
    start = jnp.zeros((cells, slots), jnp.int32)
    place = jnp.full((cells, slots), -1, jnp.int32)
    block = jnp.zeros((cells, slots), jnp.int32)
    phase_of = lane // SPAN
    group = lane - phase_of * SPAN
    for o in range(OCTANTS):
        rows = ranks[o * cells : (o + 1) * cells]
        place = jnp.where(octant == o, start + rows[:, :slots], place)
        if o:
            block = block + jnp.where(group * ROWS >= start, 1, 0)
        start = start + ((rows[:, slots:] + (ROWS - 1)) & -ROWS)
    order[...] = place
    bits = [(block >> 2) & 1, (block >> 1) & 1, block & 1]
    far_x = jnp.where(phase_of >= 2, spots[0] + 2 * bits[0], spots[0] + 1)
    far_y = jnp.where((phase_of & 1) == 1, spots[1] + 2 * bits[1], spots[1] + 1)
    table_rows[...] = (far_x * wy + far_y) * wz + spots[2] + bits[2]
    tabulate = pltpu.make_async_copy(table_rows, table, table_sem)
    tabulate.start()

    near = 1.0 - 4.0 * (own[0] * own[0] + own[1] * own[1] + own[2] * own[2])
    for k, value in enumerate([8.0 * own[0], 8.0 * own[1], 8.0 * own[2], near]):
        for part, piece in enumerate(split(value)):
            pieces_of[part, k] = piece

    batch = next(n for n in (8, 4, 2, 1) if cells % n == 0)
    kind_row = lax.broadcasted_iota(jnp.int32, (16, 4 * slots), 0)
    kind_lane = lax.broadcasted_iota(jnp.int32, (16, 4 * slots), 1)
    smear = jnp.where(
        (kind_row < 12) & ((kind_row & 3) == kind_lane // slots), 1.0, 0.0
    ).astype(jnp.bfloat16)

    def sort_cells(i, carry):
        found = []
        for j in range(batch):
            c = i * batch + j
            spot = order[pl.ds(c, 1), :]
            target = lax.broadcasted_iota(jnp.int32, (depth, slots), 0)
            pick = jnp.where(target == spot, 1.0, 0.0).astype(jnp.bfloat16)
            picks[c] = pick
            rows = [pieces_of[part, k, pl.ds(c, 1), :] for part in range(3) for k in range(4)]
            rows += [jnp.zeros((4, slots), jnp.float32)]
            found.append(
                lax.dot_general(
                    pick,
                    jnp.concatenate(rows, axis=0).astype(jnp.bfloat16),
                    (((1,), (1,)), ((), ())),
                    preferred_element_type=jnp.float32,
                ).astype(jnp.bfloat16)
            )
        for j in range(batch):
            spread = jnp.dot(found[j], smear, preferred_element_type=jnp.float32)
            for k in range(4):
                for g in range(group_count):
                    lanes_of[i * batch + j, g, k] = spread[
                        g * ROWS : (g + 1) * ROWS, k * slots : (k + 1) * slots
                    ]
        return carry

    lax.fori_loop(0, cells // batch, sort_cells, 0)

    def prepare(x, y, z, count):
        shape = (count, ROWS, slots)
        rows = [jnp.broadcast_to(ext[k, x, y, pl.ds(z, count)], shape) for k in range(3)]
        there = rows[0] < 2.0
        floor = lax.broadcasted_iota(jnp.int32, shape, 0).astype(jnp.float32) + (z - 0.5 * wz)
        shifts = (
            lax.convert_element_type(x, jnp.float32) - 0.5 * wx,
            lax.convert_element_type(y, jnp.float32) - 0.5 * wy,
            floor,
        )
        coords = [jnp.where(there, row + shift, 0.0) for row, shift in zip(rows, shifts)]
        squares = coords[0] * coords[0] + coords[1] * coords[1] + coords[2] * coords[2]
        at = pl.ds((x * wy + y) * wz + z, count)
        for k in range(3):
            far[at, k] = coords[k]
        far[at, 3] = jnp.where(there, -4.0 * squares, FAR)

    def prepare_gain(x, y, z, count):
        far_gain[pl.ds((x * wy + y) * wz + z, count)] = jnp.broadcast_to(
            gain_ext[x, y, pl.ds(z, count)], (count, ROWS, slots)
        )

    def columns(count, where, body):
        def step(i, carry):
            body(*where(i))
            return carry

        lax.fori_loop(0, count, step, 0)

    def inner_columns(body):
        columns(sx * sy, lambda i: (i // sy + 1, i % sy + 1), lambda x, y: body(x, y, 1, sz))

    def plane_columns(body):
        def ends(x, y):
            body(x, y, 0, 1)
            body(x, y, wz - 1, 1)

        columns(sx * sy, lambda i: (i // sy + 1, i % sy + 1), ends)
        columns(
            2 * sx, lambda i: (i // 2 + 1, i % 2 * (wy - 1)), lambda x, y: body(x, y, 0, wz)
        )

    def side_columns(ys, count, body):
        columns(
            2 * count,
            lambda i: (i // count * (wx - 1), ys(i % count)),
            lambda x, y: body(x, y, 0, wz),
        )

    def face_columns(body):
        side_columns(lambda y: y + 1, sy, body)

    def edge_columns(body):
        side_columns(lambda y: y * (wy - 1), 2, body)

    slot_lane = lax.broadcasted_iota(jnp.int32, (ROWS, slots), 1)

    def lane_sums(c, rows, parts):
        kept = dense[rows, :]
        for k, part in enumerate(parts):
            kept = jnp.where(
                slot_lane == k * cells + c, jnp.sum(part, axis=1, keepdims=True), kept
            )
        dense[rows, :] = kept

    def sorted_rows(kinds):
        flat = dense[...].T
        return [flat[k * cells : (k + 1) * cells, :depth] for k in range(kinds)]

    def all_cells(body, *phases):
        columns(cells, lambda i: (i,), lambda c: body(c, phases))

    def last_cells(body, *phases):
        several = next(n for n in (4, 2, 1) if cells % n == 0)

        def step(i, carry):
            for j in range(several):
                body(i * several + j, phases)
            return carry

        lax.fori_loop(0, cells // several, step, 0)

    def middle_cells(body):
        span = sz - 2
        if span > 0:
            columns(
                sx * sy * span,
                lambda i: (i // span * sz + 1 + i % span,),
                lambda c: body(c, (0,)),
            )

    def end_cells(body):
        ends = min(sz, 2)
        columns(
            ends * sx * sy,
            lambda i: (i // ends * sz + i % ends * (sz - 1),),
            lambda c: body(c, (0,)),
        )

    def density(c, phases):
        def one_group(g, inside):
            xi, yi, zi, ci = (lanes_of[c, g, k] for k in range(4))
            if phases[0]:
                rho, quartic = lanes_of[c, g, 4], lanes_of[c, g, 5]
            else:
                rho, quartic = (jnp.zeros((ROWS, slots), jnp.float32),) * 2
            for phase in phases:
                base = table[c, phase * SPAN + g]
                for step in range(2):
                    at = base + step
                    t = (far[at, 3] + ci) + xi * far[at, 0]
                    t = t + yi * far[at, 1] + zi * far[at, 2]
                    w = jnp.maximum(t, 0.0)
                    weights[c, g, 2 * phase + step] = w
                    s = w * w
                    rho = rho + s
                    quartic = quartic + s * s
            if phases[-1] == 3:
                lane_sums(c, pl.ds(g * ROWS, ROWS), (rho, quartic))
            else:
                lanes_of[c, g, 4] = rho
                lanes_of[c, g, 5] = quartic
            return inside

        lax.fori_loop(0, group_count, one_group, 0, unroll=True)

    def force(c, phases):
        def one_group(g, inside):
            gi = lanes_of[c, g, 3]
            if phases[0]:
                parts = [lanes_of[c, g, 4 + k] for k in range(4)]
            else:
                parts = [jnp.zeros((ROWS, slots), jnp.float32)] * 4
            for phase in phases:
                base = table[c, phase * SPAN + g]
                for step in range(2):
                    at = base + step
                    w = weights[c, g, 2 * phase + step]
                    f = w * ((far_gain[at] + gi) - w * w)
                    for k in range(3):
                        parts[k] = parts[k] + f * far[at, k]
                    parts[3] = parts[3] + f
            if phases[-1] == 3:
                whole = 0.125 * parts[3]
                parts = [parts[k] - lanes_of[c, g, k] * whole for k in range(3)]
                lane_sums(c, pl.ds(g * ROWS, ROWS), parts)
            else:
                for k in range(4):
                    lanes_of[c, g, 4 + k] = parts[k]
            return inside

        lax.fori_loop(0, group_count, one_group, 0, unroll=True)

    def unsort(kinds):
        pieces = [piece for value in kinds for piece in halves(value)]
        pieces = jnp.concatenate(pieces, axis=0)
        total = jnp.zeros((2 * len(kinds) * cells, slots), jnp.float32)
        row = lax.broadcasted_iota(jnp.int32, pieces.shape, 0) % cells
        for c in range(cells):
            kept = jnp.where(row == c, pieces, jnp.zeros_like(pieces))
            total = total + jnp.dot(kept, picks[c], preferred_element_type=jnp.float32)
        rows = [total[k * cells : (k + 1) * cells] for k in range(2 * len(kinds))]
        return [rows[2 * k] + rows[2 * k + 1] for k in range(len(kinds))]

    dense[...] = jnp.zeros_like(dense)
    inner_columns(prepare)
    tabulate.wait()
    middle_cells(density)
    arrive(copies, own_plane)
    plane_columns(prepare)
    end_cells(density)
    all_cells(density, 1)
    arrive(copies, side_faces)
    face_columns(prepare)
    all_cells(density, 2)
    arrive(copies, side_edges)
    edge_columns(prepare)
    last_cells(density, 3)

    rho_rows, quartic_rows = sorted_rows(2)
    first = jnp.maximum(rho_rows - 1.0, 0.0)
    second = jnp.maximum(quartic_rows - 1.0, 0.0)
    fprime = -0.5 * EMBED_SCALE * lax.rsqrt(first + 1.0)
    gain = 0.5 - fprime * (0.5 / PAIR_SCALE)
    gain_rows = unsort([gain])[0]
    gain_own[...] = gain_rows.reshape(sizes + (1, slots))
    copies = send_rims(mesh_counts, gain_own, gain_ext, gain_sent, gain_landed)
    gain_ext[inner] = gain_rows.reshape(sizes + (1, slots))
    pair_sum = PAIR_SCALE * (second - 2.0 * first)
    energy = -EMBED_SCALE * jnp.sqrt(first + 1.0) + 0.5 * pair_sum
    energy_rows = unsort([energy])[0]
    energy_ref[...] = jnp.where(filled, energy_rows, 0.0).reshape(sizes + (slots,))

    tall = [piece.astype(jnp.float32) for piece in halves(gain)]
    tall += [jnp.zeros((slots - 2 * cells, depth), jnp.float32)]
    tall = jnp.concatenate(tall, axis=0)
    tall = jnp.concatenate([tall, jnp.zeros((slots, -depth % 128), jnp.float32)], axis=1)
    standing = tall.T[:depth].astype(jnp.bfloat16)
    pair = 2 if cells % 2 == 0 else 1
    pick_row = lax.broadcasted_iota(jnp.int32, (slots, pair * slots), 0)
    pick_cell = jnp.where(
        pick_row < 2 * cells, pick_row - jnp.where(pick_row >= cells, cells, 0), -1
    )
    pick_lane = lax.broadcasted_iota(jnp.int32, (slots, pair * slots), 1) // slots
    for i in range(cells // pair):
        chosen = jnp.where(pick_cell == pair * i + pick_lane, 1.0, 0.0).astype(jnp.bfloat16)
        spread = jnp.dot(standing, chosen, preferred_element_type=jnp.float32)
        for j in range(pair):
            for g in range(group_count):
                lanes_of[pair * i + j, g, 3] = spread[
                    g * ROWS : (g + 1) * ROWS, j * slots : (j + 1) * slots
                ]

    inner_columns(prepare_gain)
    middle_cells(force)
    arrive(copies, own_plane)
    plane_columns(prepare_gain)
    end_cells(force)
    all_cells(force, 1)
    arrive(copies, side_faces)
    arrive(copies, side_edges)
    face_columns(prepare_gain)
    edge_columns(prepare_gain)
    last_cells(force, 2, 3)

    scale = FORCE_SCALE * 4.0 * PAIR_SCALE
    for k, push in enumerate(unsort(sorted_rows(3))):
        force_ref[k] = jnp.where(filled, scale * push, 0.0).reshape(sizes + (slots,))


def per_device(mesh_counts, positions, counts):
    slots = positions.shape[-1]
    sizes = positions.shape[1:4]
    wide = tuple(size + 2 for size in sizes)
    cells = sizes[0] * sizes[1] * sizes[2]
    far_cells = wide[0] * wide[1] * wide[2]
    groups = (slots + OCTANTS * (ROWS - 1)) // ROWS
    depth = -(-groups // 2) * 2 * ROWS
    f32, bf16, i32 = jnp.float32, jnp.bfloat16, jnp.int32
    vmem = [
        ((3,) + sizes + (slots,), f32),
        ((3,) + sizes + (1, slots), f32),
        ((3,) + wide + (1, slots), f32),
        ((far_cells, 4, ROWS, slots), f32),
        ((far_cells, ROWS, slots), f32),
        (sizes + (1, slots), f32),
        (wide + (1, slots), f32),
        ((cells, slots), i32),
        ((3, 4, cells, slots), f32),
        ((cells, depth, slots), bf16),
        ((cells, groups, 8, ROWS, slots), f32),
        ((cells, groups, 8, ROWS, slots), f32),
        ((-(-depth // 128) * 128, slots), f32),
        ((cells, slots), i32),
    ]
    held = sum(math.prod(shape) * jnp.dtype(kind).itemsize for shape, kind in vmem)
    return pl.pallas_call(
        functools.partial(kernel, mesh_counts),
        out_shape=(
            jax.ShapeDtypeStruct(sizes + (slots,), f32),
            jax.ShapeDtypeStruct((3,) + sizes + (slots,), f32),
        ),
        in_specs=[pl.BlockSpec(memory_space=pltpu.HBM)] * 2,
        out_specs=(pl.BlockSpec(memory_space=pltpu.VMEM),) * 2,
        scratch_shapes=[pltpu.SMEM(counts.shape, i32)]
        + [pltpu.VMEM(shape, kind) for shape, kind in vmem]
        + [
            pltpu.SMEM((cells, slots), i32),
            pltpu.SemaphoreType.DMA((2,)),
            pltpu.SemaphoreType.DMA,
        ]
        + [pltpu.SemaphoreType.DMA((len(DIRECTIONS),))] * 4,
        compiler_params=pltpu.CompilerParams(
            collective_id=0,
            has_side_effects=True,
            vmem_limit_bytes=held + (4 << 20),
        ),
        name="atoms",
    )(*(pltpu.with_memory_space_constraint(x, pltpu.HBM) for x in (counts, positions)))


def solution(mesh):
    placed = (P(None, "gx", "gy", "gz", None), P("gx", "gy", "gz"))
    return jax.shard_map(
        functools.partial(per_device, tuple(mesh.shape[name] for name in NAMES)),
        mesh=mesh,
        in_specs=placed,
        out_specs=(P("gx", "gy", "gz", None), P(None, "gx", "gy", "gz", None)),
        check_vma=False,
    )
```

time: 34.3 us -> 28.6 us (0.83)
  Pallas kernels: 30.7 us -> 26.6 us
  local copies, waits for them, and re-layouts: 2.64 us -> 1.21 us
    pallas_call x1, Pallas kernels: 30.7 us -> 26.6 us  [per_device(): pl.pallas_call(functools.partial(kernel, mesh_counts), out_shape=(jax.Sha...]
    unnamed x2, local copies, waits for them, and re-layouts: 2.64 us -> 1.21 us
where the time goes in v2:
time: 28.6 us; the launch traced here: 28.4 us
  Pallas kernels  26.6 us (93%)
  local copies, waits for them, and re-layouts  1.21 us (4%)
  between operations  0.64 us (2%)
    pallas_call x1, Pallas kernels, per_device(): pl.pallas_call(functools.partial(kernel, mesh_counts), out_shape=(jax.Sha...  26.6 us
    unnamed x2, local copies, waits for them, and re-layouts  1.21 us

profile of v2, /device:TPU:0, one launch (start us, length us, event | category | flops | bytes accessed | tf_op | source)
XLA Modules:
  0.0 28.4 jit_solution(2253294512464045234)
XLA Ops:
  0.6 26.6 %atoms.1 = (f32[1,2,8,128]{3,2,1,0:T(8,128)S(1)}, f32[3,1,2,8,128]{4,3,2,1,0:T(8,128)S(1)}) custom-call(s32[1,2,8]{2,1,0:T(2,128)} %counts.1, f32[3,1,2,8,128]{4,3,2,1,0:T(8,128)} %positions.1), custom_call_target="tpu_custom_call" | custom-call | tf_op jit(solution)/shard_map/atoms/pallas_call | solution.py:517
  27.2 0.6 %copy.6 = f32[1,2,8,128]{3,2,1,0:T(8,128)} copy(f32[1,2,8,128]{3,2,1,0:T(8,128)S(1)} %get-tuple-element.4) | data formatting | bytes 16384
  27.8 0.6 %copy.7 = f32[3,1,2,8,128]{4,3,2,1,0:T(8,128)} copy(f32[3,1,2,8,128]{4,3,2,1,0:T(8,128)S(1)} %get-tuple-element.5) | data formatting | bytes 49152

commit v3 on v2

--- a/solution.py
+++ b/solution.py
@@ -58,11 +58,14 @@
     pl.semaphore_wait(pltpu.get_barrier_semaphore(), len(partners(counts)))
 
 
+def kind_of(step):
+    return (2 if step[0] else 0) + (1 if step[1] else 0)
+
+
 def send_rims(counts, source, target, sent, landed):
     lead = (slice(None),) * (source.ndim - 5)
     sizes = source.shape[-5:-2]
-    copies = []
-    for at, step in enumerate(DIRECTIONS):
+    for step in DIRECTIONS:
         here = tuple(
             pl.ds(0, size) if o == 0 else pl.ds(size - 1 if o > 0 else 0, 1)
             for o, size in zip(step, sizes)
@@ -71,35 +74,23 @@
             pl.ds(1, size) if o == 0 else pl.ds(0 if o > 0 else size + 1, 1)
             for o, size in zip(step, sizes)
         )
-        copy = pltpu.make_async_remote_copy(
+        pltpu.make_async_remote_copy(
             src_ref=source.at[lead + here],
             dst_ref=target.at[lead + there],
-            send_sem=sent.at[at],
-            recv_sem=landed.at[at],
+            send_sem=sent.at[kind_of(step)],
+            recv_sem=landed.at[kind_of(step)],
             device_id=device_at(counts, step),
             device_id_type=pl.DeviceIdType.MESH,
-        )
-        copy.start()
-        copies.append(copy)
-    return copies
-
-
-def arrive(copies, chosen):
-    for step, copy in zip(DIRECTIONS, copies):
-        if chosen(step):
-            copy.wait()
-
-
-def own_plane(step):
-    return step[0] == 0
-
-
-def side_faces(step):
-    return step[0] != 0 and step[1] == 0
-
-
-def side_edges(step):
-    return step[0] != 0 and step[1] != 0
+        ).start()
+
+
+def arrive(kind, target, sizes, sent, landed):
+    sx, sy, _ = sizes
+    lead = (slice(None),) * (target.ndim - 5)
+    extent = ((sx, sy, 2), (sx, 2, sizes[2] + 2), (2, sy, sizes[2] + 2), (2, 2, sizes[2] + 2))[kind]
+    whole = target.at[lead + tuple(pl.ds(0, size) for size in extent)]
+    pltpu.make_async_copy(whole, whole, sent.at[kind]).wait()
+    pltpu.make_async_copy(whole, whole, landed.at[kind]).wait()
 
 
 def halves(value):
@@ -118,7 +109,6 @@
     source,
     ext,
     far,
-    far_gain,
     gain_own,
     gain_ext,
     order,
@@ -127,13 +117,13 @@
     weights,
     lanes_of,
     dense,
+    piles,
     table_rows,
     table,
     fetch_sem,
     table_sem,
     sent,
     landed,
-    gain_sent,
     gain_landed,
 ):
     sizes = gain_own.shape[:3]
@@ -175,7 +165,7 @@
         source[k] = seated[k].reshape(sizes + (1, slots))
 
     meet(mesh_counts)
-    copies = send_rims(mesh_counts, source, ext, sent, landed)
+    send_rims(mesh_counts, source, ext, sent, landed)
 
     own = [
         jnp.where(
@@ -259,8 +249,8 @@
     lax.fori_loop(0, cells // batch, sort_cells, 0)
 
     def prepare(x, y, z, count):
-        shape = (count, ROWS, slots)
-        rows = [jnp.broadcast_to(ext[k, x, y, pl.ds(z, count)], shape) for k in range(3)]
+        shape = (count, 1, slots)
+        rows = [ext[k, x, y, pl.ds(z, count)] for k in range(3)]
         there = rows[0] < 2.0
         floor = lax.broadcasted_iota(jnp.int32, shape, 0).astype(jnp.float32) + (z - 0.5 * wz)
         shifts = (
@@ -272,13 +262,14 @@
         squares = coords[0] * coords[0] + coords[1] * coords[1] + coords[2] * coords[2]
         at = pl.ds((x * wy + y) * wz + z, count)
         for k in range(3):
-            far[at, k] = coords[k]
-        far[at, 3] = jnp.where(there, -4.0 * squares, FAR)
+            far[at, k : k + 1] = coords[k]
+        far[at, 3:4] = jnp.where(there, -4.0 * squares, FAR)
 
     def prepare_gain(x, y, z, count):
-        far_gain[pl.ds((x * wy + y) * wz + z, count)] = jnp.broadcast_to(
-            gain_ext[x, y, pl.ds(z, count)], (count, ROWS, slots)
-        )
+        far[pl.ds((x * wy + y) * wz + z, count), 4:5] = gain_ext[x, y, pl.ds(z, count)]
+
+    def far_row(at, k):
+        return jnp.broadcast_to(far[at, k : k + 1], (ROWS, slots))
 
     def columns(count, where, body):
         def step(i, carry):
@@ -290,12 +281,14 @@
     def inner_columns(body):
         columns(sx * sy, lambda i: (i // sy + 1, i % sy + 1), lambda x, y: body(x, y, 1, sz))
 
-    def plane_columns(body):
+    def end_columns(body):
         def ends(x, y):
             body(x, y, 0, 1)
             body(x, y, wz - 1, 1)
 
         columns(sx * sy, lambda i: (i // sy + 1, i % sy + 1), ends)
+
+    def plane_columns(body):
         columns(
             2 * sx, lambda i: (i // 2 + 1, i % 2 * (wy - 1)), lambda x, y: body(x, y, 0, wz)
         )
@@ -327,27 +320,26 @@
         flat = dense[...].T
         return [flat[k * cells : (k + 1) * cells, :depth] for k in range(kinds)]
 
-    def all_cells(body, *phases):
-        columns(cells, lambda i: (i,), lambda c: body(c, phases))
-
-    def last_cells(body, *phases):
-        several = next(n for n in (4, 2, 1) if cells % n == 0)
+    def batched(count, most, where, body, phases):
+        several = next(n for n in range(most, 0, -1) if count % n == 0)
 
         def step(i, carry):
             for j in range(several):
-                body(i * several + j, phases)
+                body(where(i * several + j), phases)
             return carry
 
-        lax.fori_loop(0, cells // several, step, 0)
+        lax.fori_loop(0, count // several, step, 0)
+
+    def all_cells(body, *phases):
+        batched(cells, 2, lambda i: i, body, phases)
+
+    def last_cells(body, *phases):
+        batched(cells, 4, lambda i: i, body, phases)
 
     def middle_cells(body):
         span = sz - 2
         if span > 0:
-            columns(
-                sx * sy * span,
-                lambda i: (i // span * sz + 1 + i % span,),
-                lambda c: body(c, (0,)),
-            )
+            batched(sx * sy * span, 2, lambda i: i // span * sz + 1 + i % span, body, (0,))
 
     def end_cells(body):
         ends = min(sz, 2)
@@ -368,8 +360,8 @@
                 base = table[c, phase * SPAN + g]
                 for step in range(2):
                     at = base + step
-                    t = (far[at, 3] + ci) + xi * far[at, 0]
-                    t = t + yi * far[at, 1] + zi * far[at, 2]
+                    t = (far_row(at, 3) + ci) + xi * far_row(at, 0)
+                    t = t + yi * far_row(at, 1) + zi * far_row(at, 2)
                     w = jnp.maximum(t, 0.0)
                     weights[c, g, 2 * phase + step] = w
                     s = w * w
@@ -396,9 +388,9 @@
                 for step in range(2):
                     at = base + step
                     w = weights[c, g, 2 * phase + step]
-                    f = w * ((far_gain[at] + gi) - w * w)
+                    f = w * ((far_row(at, 4) + gi) - w * w)
                     for k in range(3):
-                        parts[k] = parts[k] + f * far[at, k]
+                        parts[k] = parts[k] + f * far_row(at, k)
                     parts[3] = parts[3] + f
             if phases[-1] == 3:
                 whole = 0.125 * parts[3]
@@ -414,26 +406,48 @@
     def unsort(kinds):
         pieces = [piece for value in kinds for piece in halves(value)]
         pieces = jnp.concatenate(pieces, axis=0)
-        total = jnp.zeros((2 * len(kinds) * cells, slots), jnp.float32)
+        tall = pieces.shape[0]
         row = lax.broadcasted_iota(jnp.int32, pieces.shape, 0) % cells
-        for c in range(cells):
-            kept = jnp.where(row == c, pieces, jnp.zeros_like(pieces))
-            total = total + jnp.dot(kept, picks[c], preferred_element_type=jnp.float32)
+        for lot in range(lots):
+            total = jnp.zeros((tall, pair * slots), jnp.float32)
+            for c in range(lot * cells // lots, (lot + 1) * cells // lots, pair):
+                kept = jnp.where((row >= c) & (row < c + pair), pieces, jnp.zeros_like(pieces))
+                both = jnp.concatenate([picks[c + j] for j in range(pair)], axis=1)
+                total = total + jnp.dot(kept, both, preferred_element_type=jnp.float32)
+            piles[lot, :tall] = total
+        total = sum(piles[lot, :tall] for lot in range(lots))
+        odd = lax.broadcasted_iota(jnp.int32, (tall, slots), 0) % pair
+        total = functools.reduce(
+            lambda kept, j: jnp.where(odd == j, total[:, j * slots : (j + 1) * slots], kept),
+            range(1, pair),
+            total[:, :slots],
+        )
         rows = [total[k * cells : (k + 1) * cells] for k in range(2 * len(kinds))]
         return [rows[2 * k] + rows[2 * k + 1] for k in range(len(kinds))]
+
+    pair = 2 if cells % 2 == 0 else 1
+    lots = 2 if cells % 4 == 0 else 1
+
+    def land(kind):
+        arrive(kind, ext, sizes, sent, landed)
+
+    def land_gain(kind):
+        arrive(kind, gain_ext, sizes, sent, gain_landed)
 
     dense[...] = jnp.zeros_like(dense)
     inner_columns(prepare)
     tabulate.wait()
     middle_cells(density)
-    arrive(copies, own_plane)
+    land(0)
+    end_columns(prepare)
+    end_cells(density)
+    land(1)
     plane_columns(prepare)
-    end_cells(density)
     all_cells(density, 1)
-    arrive(copies, side_faces)
+    land(2)
     face_columns(prepare)
     all_cells(density, 2)
-    arrive(copies, side_edges)
+    land(3)
     edge_columns(prepare)
     last_cells(density, 3)
 
@@ -444,7 +458,7 @@
     gain = 0.5 - fprime * (0.5 / PAIR_SCALE)
     gain_rows = unsort([gain])[0]
     gain_own[...] = gain_rows.reshape(sizes + (1, slots))
-    copies = send_rims(mesh_counts, gain_own, gain_ext, gain_sent, gain_landed)
+    send_rims(mesh_counts, gain_own, gain_ext, sent, gain_landed)
     gain_ext[inner] = gain_rows.reshape(sizes + (1, slots))
     pair_sum = PAIR_SCALE * (second - 2.0 * first)
     energy = -EMBED_SCALE * jnp.sqrt(first + 1.0) + 0.5 * pair_sum
@@ -456,7 +470,6 @@
     tall = jnp.concatenate(tall, axis=0)
     tall = jnp.concatenate([tall, jnp.zeros((slots, -depth % 128), jnp.float32)], axis=1)
     standing = tall.T[:depth].astype(jnp.bfloat16)
-    pair = 2 if cells % 2 == 0 else 1
     pick_row = lax.broadcasted_iota(jnp.int32, (slots, pair * slots), 0)
     pick_cell = jnp.where(
         pick_row < 2 * cells, pick_row - jnp.where(pick_row >= cells, cells, 0), -1
@@ -473,18 +486,21 @@
 
     inner_columns(prepare_gain)
     middle_cells(force)
-    arrive(copies, own_plane)
+    land_gain(0)
+    end_columns(prepare_gain)
+    end_cells(force)
+    land_gain(1)
     plane_columns(prepare_gain)
-    end_cells(force)
     all_cells(force, 1)
-    arrive(copies, side_faces)
-    arrive(copies, side_edges)
+    land_gain(2)
     face_columns(prepare_gain)
+    land_gain(3)
     edge_columns(prepare_gain)
     last_cells(force, 2, 3)
 
     scale = FORCE_SCALE * 4.0 * PAIR_SCALE
-    for k, push in enumerate(unsort(sorted_rows(3))):
+    pushes = unsort(sorted_rows(3))
+    for k, push in enumerate(pushes):
         force_ref[k] = jnp.where(filled, scale * push, 0.0).reshape(sizes + (slots,))
 
 
@@ -501,7 +517,6 @@
         ((3,) + sizes + (slots,), f32),
         ((3,) + sizes + (1, slots), f32),
         ((3,) + wide + (1, slots), f32),
-        ((far_cells, 4, ROWS, slots), f32),
         ((far_cells, ROWS, slots), f32),
         (sizes + (1, slots), f32),
         (wide + (1, slots), f32),
@@ -511,6 +526,7 @@
         ((cells, groups, 8, ROWS, slots), f32),
         ((cells, groups, 8, ROWS, slots), f32),
         ((-(-depth // 128) * 128, slots), f32),
+        ((2, 6 * cells, 2 * slots), f32),
         ((cells, slots), i32),
     ]
     held = sum(math.prod(shape) * jnp.dtype(kind).itemsize for shape, kind in vmem)
@@ -529,7 +545,7 @@
             pltpu.SemaphoreType.DMA((2,)),
             pltpu.SemaphoreType.DMA,
         ]
-        + [pltpu.SemaphoreType.DMA((len(DIRECTIONS),))] * 4,
+        + [pltpu.SemaphoreType.DMA((4,))] * 3,
         compiler_params=pltpu.CompilerParams(
             collective_id=0,
             has_side_effects=True,

time: 28.6 us -> 25.9 us (0.906)
  Pallas kernels: 26.6 us -> 23.9 us
    pallas_call x1, Pallas kernels: 26.6 us -> 23.9 us  [per_device(): pl.pallas_call(functools.partial(kernel, mesh_counts), out_shape=(jax.Sha...]
where the time goes in v3:
time: 25.9 us; the launch traced here: 25.8 us
  Pallas kernels  23.9 us (92%)
  local copies, waits for them, and re-layouts  1.21 us (5%)
  between operations  0.64 us (2%)
    pallas_call x1, Pallas kernels, per_device(): pl.pallas_call(functools.partial(kernel, mesh_counts), out_shape=(jax.Sha...  23.9 us
    unnamed x2, local copies, waits for them, and re-layouts  1.21 us

profile of v3, /device:TPU:0, one launch (start us, length us, event | category | flops | bytes accessed | tf_op | source)
XLA Modules:
  0.0 25.8 jit_solution(6523516943062226536)
XLA Ops:
  0.6 23.9 %atoms.1 = (f32[1,2,8,128]{3,2,1,0:T(8,128)S(1)}, f32[3,1,2,8,128]{4,3,2,1,0:T(8,128)S(1)}) custom-call(s32[1,2,8]{2,1,0:T(2,128)} %counts.1, f32[3,1,2,8,128]{4,3,2,1,0:T(8,128)} %positions.1), custom_call_target="tpu_custom_call" | custom-call | tf_op jit(solution)/shard_map/atoms/pallas_call | solution.py:533
  24.6 0.6 %copy.6 = f32[1,2,8,128]{3,2,1,0:T(8,128)} copy(f32[1,2,8,128]{3,2,1,0:T(8,128)S(1)} %get-tuple-element.4) | data formatting | bytes 16384
  25.2 0.6 %copy.7 = f32[3,1,2,8,128]{4,3,2,1,0:T(8,128)} copy(f32[3,1,2,8,128]{4,3,2,1,0:T(8,128)S(1)} %get-tuple-element.5) | data formatting | bytes 49152

commit v4 on v3

--- a/solution.py
+++ b/solution.py
@@ -40,7 +40,10 @@
 
 
 def partners(counts):
-    return sorted({tuple(o % c for o, c in zip(step, counts)) for step in DIRECTIONS})
+    return sorted(
+        {tuple(o % c for o, c in zip(step, counts)) for step in DIRECTIONS},
+        key=lambda step: [-min(o, c - o) for o, c in zip(step, counts)],
+    )
 
 
 def greet(counts):
@@ -164,8 +167,6 @@
     for k in range(3):
         source[k] = seated[k].reshape(sizes + (1, slots))
 
-    meet(mesh_counts)
-    send_rims(mesh_counts, source, ext, sent, landed)
 
     own = [
         jnp.where(
@@ -247,6 +248,8 @@
         return carry
 
     lax.fori_loop(0, cells // batch, sort_cells, 0)
+    meet(mesh_counts)
+    send_rims(mesh_counts, source, ext, sent, landed)
 
     def prepare(x, y, z, count):
         shape = (count, 1, slots)
@@ -331,10 +334,10 @@
         lax.fori_loop(0, count // several, step, 0)
 
     def all_cells(body, *phases):
-        batched(cells, 2, lambda i: i, body, phases)
+        batched(cells, 4, lambda i: i, body, phases)
 
     def last_cells(body, *phases):
-        batched(cells, 4, lambda i: i, body, phases)
+        batched(cells, 8, lambda i: i, body, phases)
 
     def middle_cells(body):
         span = sz - 2
@@ -502,6 +505,17 @@
     pushes = unsort(sorted_rows(3))
     for k, push in enumerate(pushes):
         force_ref[k] = jnp.where(filled, scale * push, 0.0).reshape(sizes + (slots,))
+
+
+def hand_over(energy, force, energy_out, force_out, done):
+    copies = [
+        pltpu.make_async_copy(force, force_out, done.at[0]),
+        pltpu.make_async_copy(energy, energy_out, done.at[1]),
+    ]
+    for copy in copies:
+        copy.start()
+    for copy in copies:
+        copy.wait()
 
 
 def per_device(mesh_counts, positions, counts):
@@ -530,7 +544,7 @@
         ((cells, slots), i32),
     ]
     held = sum(math.prod(shape) * jnp.dtype(kind).itemsize for shape, kind in vmem)
-    return pl.pallas_call(
+    results = pl.pallas_call(
         functools.partial(kernel, mesh_counts),
         out_shape=(
             jax.ShapeDtypeStruct(sizes + (slots,), f32),
@@ -553,6 +567,15 @@
         ),
         name="atoms",
     )(*(pltpu.with_memory_space_constraint(x, pltpu.HBM) for x in (counts, positions)))
+    return pl.pallas_call(
+        hand_over,
+        out_shape=tuple(jax.ShapeDtypeStruct(x.shape, x.dtype) for x in results),
+        in_specs=[pl.BlockSpec(memory_space=pltpu.VMEM)] * 2,
+        out_specs=(pl.BlockSpec(memory_space=pl.ANY),) * 2,
+        scratch_shapes=[pltpu.SemaphoreType.DMA((2,))],
+        compiler_params=pltpu.CompilerParams(vmem_limit_bytes=1 << 20),
+        name="hand",
+    )(*results)
 
 
 def solution(mesh):

time: 25.9 us -> 24.8 us (0.958)
  local copies, waits for them, and re-layouts: 1.21 us -> 0 us
    unnamed x2 -> x0, local copies, waits for them, and re-layouts: 1.21 us -> none
    pallas_call x0 -> x1, Pallas kernels: none -> 0.63 us  [per_device(): pl.pallas_call(hand_over, out_shape=tuple((jax.ShapeDtypeStruct(x.shape,...]
    pallas_call x1, Pallas kernels: 23.9 us -> 23.3 us  [per_device(): pl.pallas_call(functools.partial(kernel, mesh_counts), out_shape=(jax.Sha...]
where the time goes in v4:
time: 24.8 us; the launch traced here: 24.6 us
  Pallas kernels  23.9 us (96%)
  between operations  0.64 us (3%)
    pallas_call x1, Pallas kernels, per_device(): pl.pallas_call(functools.partial(kernel, mesh_counts), out_shape=(jax.Sha...  23.3 us
    pallas_call x1, Pallas kernels, per_device(): pl.pallas_call(hand_over, out_shape=tuple((jax.ShapeDtypeStruct(x.shape,...  0.63 us

profile of v4, /device:TPU:0, one launch (start us, length us, event | category | flops | bytes accessed | tf_op | source)
XLA Modules:
  0.0 24.6 jit_solution(8972318732005270534)
XLA Ops:
  0.6 23.3 %atoms.1 = (f32[1,2,8,128]{3,2,1,0:T(8,128)S(1)}, f32[3,1,2,8,128]{4,3,2,1,0:T(8,128)S(1)}) custom-call(s32[1,2,8]{2,1,0:T(2,128)} %counts.1, f32[3,1,2,8,128]{4,3,2,1,0:T(8,128)} %positions.1), custom_call_target="tpu_custom_call" | custom-call | tf_op jit(solution)/shard_map/atoms/pallas_call | solution.py:547
  24.0 0.6 %hand.1 = (f32[1,2,8,128]{3,2,1,0:T(8,128)}, f32[3,1,2,8,128]{4,3,2,1,0:T(8,128)}) custom-call(f32[1,2,8,128]{3,2,1,0:T(8,128)S(1)} %get-tuple-element.4.energy, f32[3,1,2,8,128]{4,3,2,1,0:T(8,128)S(1)} %get-tuple-element.5.force), custom_call_target="tpu_custom_call" | custom-call | tf_op jit(solution)/shard_map/hand/pallas_call | solution.py:570

commit v5 on v4

--- a/solution.py
+++ b/solution.py
@@ -16,6 +16,7 @@
 ROWS = 8
 OCTANTS = 8
 SPAN = 32
+SLOTS = 8
 
 
 def split(value):
@@ -111,12 +112,12 @@
     raw,
     source,
     ext,
-    far,
     gain_own,
     gain_ext,
     order,
     pieces_of,
     picks,
+    far,
     weights,
     lanes_of,
     dense,
@@ -135,9 +136,12 @@
     wx, wy, wz = wide
     slots = source.shape[-1]
     cells = sx * sy * sz
-    group_count = weights.shape[1]
+    group_count = groups_of(slots)
     depth = picks.shape[1]
-    plane = wy * wz
+    each = -(-SLOTS // weights.shape[2])
+
+    def held_at(c, g, i):
+        return c, g, i // each, i % each
 
     fetches = [
         pltpu.make_async_copy(counts, held, fetch_sem.at[0]),
@@ -242,7 +246,7 @@
             spread = jnp.dot(found[j], smear, preferred_element_type=jnp.float32)
             for k in range(4):
                 for g in range(group_count):
-                    lanes_of[i * batch + j, g, k] = spread[
+                    lanes_of[held_at(i * batch + j, g, k)] = spread[
                         g * ROWS : (g + 1) * ROWS, k * slots : (k + 1) * slots
                     ]
         return carry
@@ -265,14 +269,14 @@
         squares = coords[0] * coords[0] + coords[1] * coords[1] + coords[2] * coords[2]
         at = pl.ds((x * wy + y) * wz + z, count)
         for k in range(3):
-            far[at, k : k + 1] = coords[k]
-        far[at, 3:4] = jnp.where(there, -4.0 * squares, FAR)
+            far[at, 3, k : k + 1] = coords[k]
+        far[at, 3, 3:4] = jnp.where(there, -4.0 * squares, FAR)
 
     def prepare_gain(x, y, z, count):
-        far[pl.ds((x * wy + y) * wz + z, count), 4:5] = gain_ext[x, y, pl.ds(z, count)]
+        far[pl.ds((x * wy + y) * wz + z, count), 3, 4:5] = gain_ext[x, y, pl.ds(z, count)]
 
     def far_row(at, k):
-        return jnp.broadcast_to(far[at, k : k + 1], (ROWS, slots))
+        return jnp.broadcast_to(far[at, 3, k : k + 1], (ROWS, slots))
 
     def columns(count, where, body):
         def step(i, carry):
@@ -354,9 +358,9 @@
 
     def density(c, phases):
         def one_group(g, inside):
-            xi, yi, zi, ci = (lanes_of[c, g, k] for k in range(4))
+            xi, yi, zi, ci = (lanes_of[held_at(c, g, k)] for k in range(4))
             if phases[0]:
-                rho, quartic = lanes_of[c, g, 4], lanes_of[c, g, 5]
+                rho, quartic = lanes_of[held_at(c, g, 4)], lanes_of[held_at(c, g, 5)]
             else:
                 rho, quartic = (jnp.zeros((ROWS, slots), jnp.float32),) * 2
             for phase in phases:
@@ -366,42 +370,42 @@
                     t = (far_row(at, 3) + ci) + xi * far_row(at, 0)
                     t = t + yi * far_row(at, 1) + zi * far_row(at, 2)
                     w = jnp.maximum(t, 0.0)
-                    weights[c, g, 2 * phase + step] = w
+                    weights[held_at(c, g, 2 * phase + step)] = w
                     s = w * w
                     rho = rho + s
                     quartic = quartic + s * s
             if phases[-1] == 3:
                 lane_sums(c, pl.ds(g * ROWS, ROWS), (rho, quartic))
             else:
-                lanes_of[c, g, 4] = rho
-                lanes_of[c, g, 5] = quartic
+                lanes_of[held_at(c, g, 4)] = rho
+                lanes_of[held_at(c, g, 5)] = quartic
             return inside
 
         lax.fori_loop(0, group_count, one_group, 0, unroll=True)
 
     def force(c, phases):
         def one_group(g, inside):
-            gi = lanes_of[c, g, 3]
+            gi = lanes_of[held_at(c, g, 3)]
             if phases[0]:
-                parts = [lanes_of[c, g, 4 + k] for k in range(4)]
+                parts = [lanes_of[held_at(c, g, 4 + k)] for k in range(4)]
             else:
                 parts = [jnp.zeros((ROWS, slots), jnp.float32)] * 4
             for phase in phases:
                 base = table[c, phase * SPAN + g]
                 for step in range(2):
                     at = base + step
-                    w = weights[c, g, 2 * phase + step]
+                    w = weights[held_at(c, g, 2 * phase + step)]
                     f = w * ((far_row(at, 4) + gi) - w * w)
                     for k in range(3):
                         parts[k] = parts[k] + f * far_row(at, k)
                     parts[3] = parts[3] + f
             if phases[-1] == 3:
                 whole = 0.125 * parts[3]
-                parts = [parts[k] - lanes_of[c, g, k] * whole for k in range(3)]
+                parts = [parts[k] - lanes_of[held_at(c, g, k)] * whole for k in range(3)]
                 lane_sums(c, pl.ds(g * ROWS, ROWS), parts)
             else:
                 for k in range(4):
-                    lanes_of[c, g, 4 + k] = parts[k]
+                    lanes_of[held_at(c, g, 4 + k)] = parts[k]
             return inside
 
         lax.fori_loop(0, group_count, one_group, 0, unroll=True)
@@ -483,7 +487,7 @@
         spread = jnp.dot(standing, chosen, preferred_element_type=jnp.float32)
         for j in range(pair):
             for g in range(group_count):
-                lanes_of[pair * i + j, g, 3] = spread[
+                lanes_of[held_at(pair * i + j, g, 3)] = spread[
                     g * ROWS : (g + 1) * ROWS, j * slots : (j + 1) * slots
                 ]
 
@@ -507,6 +511,10 @@
         force_ref[k] = jnp.where(filled, scale * push, 0.0).reshape(sizes + (slots,))
 
 
+def groups_of(slots):
+    return (slots + OCTANTS * (ROWS - 1)) // ROWS
+
+
 def hand_over(energy, force, energy_out, force_out, done):
     copies = [
         pltpu.make_async_copy(force, force_out, done.at[0]),
@@ -524,21 +532,23 @@
     wide = tuple(size + 2 for size in sizes)
     cells = sizes[0] * sizes[1] * sizes[2]
     far_cells = wide[0] * wide[1] * wide[2]
-    groups = (slots + OCTANTS * (ROWS - 1)) // ROWS
+    groups = groups_of(slots)
     depth = -(-groups // 2) * 2 * ROWS
     f32, bf16, i32 = jnp.float32, jnp.bfloat16, jnp.int32
+    roomy = 2 * cells * groups * -(-SLOTS // 3) * 16 * ROWS * slots <= 40 << 20
+    quads = -(-SLOTS // (3 if roomy else 4))
     vmem = [
         ((3,) + sizes + (slots,), f32),
         ((3,) + sizes + (1, slots), f32),
         ((3,) + wide + (1, slots), f32),
-        ((far_cells, ROWS, slots), f32),
         (sizes + (1, slots), f32),
         (wide + (1, slots), f32),
         ((cells, slots), i32),
         ((3, 4, cells, slots), f32),
         ((cells, depth, slots), bf16),
-        ((cells, groups, 8, ROWS, slots), f32),
-        ((cells, groups, 8, ROWS, slots), f32),
+        ((far_cells, 4, ROWS, slots), f32),
+        ((cells, groups, quads, 4, ROWS, slots), f32),
+        ((cells, groups, quads, 4, ROWS, slots), f32),
         ((-(-depth // 128) * 128, slots), f32),
         ((2, 6 * cells, 2 * slots), f32),
         ((cells, slots), i32),

time: 24.8 us -> 23.8 us (0.960)
  Pallas kernels: 23.9 us -> 23 us
    pallas_call x1, Pallas kernels: 23.3 us -> 22.3 us  [per_device(): pl.pallas_call(functools.partial(kernel, mesh_counts), out_shape=(jax.Sha...]
where the time goes in v5:
time: 23.8 us; the launch traced here: 23.6 us
  Pallas kernels  23 us (97%)
  between operations  0.64 us (3%)
    pallas_call x1, Pallas kernels, per_device(): pl.pallas_call(functools.partial(kernel, mesh_counts), out_shape=(jax.Sha...  22.3 us
    pallas_call x1, Pallas kernels, per_device(): pl.pallas_call(hand_over, out_shape=tuple((jax.ShapeDtypeStruct(x.shape,...  0.63 us

profile of v5, /device:TPU:0, one launch (start us, length us, event | category | flops | bytes accessed | tf_op | source)
XLA Modules:
  0.0 23.6 jit_solution(13534354082604344546)
XLA Ops:
  0.6 22.3 %atoms.1 = (f32[1,2,8,128]{3,2,1,0:T(8,128)S(1)}, f32[3,1,2,8,128]{4,3,2,1,0:T(8,128)S(1)}) custom-call(s32[1,2,8]{2,1,0:T(2,128)} %counts.1, f32[3,1,2,8,128]{4,3,2,1,0:T(8,128)} %positions.1), custom_call_target="tpu_custom_call" | custom-call | tf_op jit(solution)/shard_map/atoms/pallas_call | solution.py:557
  23.0 0.6 %hand.1 = (f32[1,2,8,128]{3,2,1,0:T(8,128)}, f32[3,1,2,8,128]{4,3,2,1,0:T(8,128)}) custom-call(f32[1,2,8,128]{3,2,1,0:T(8,128)S(1)} %get-tuple-element.4.energy, f32[3,1,2,8,128]{4,3,2,1,0:T(8,128)S(1)} %get-tuple-element.5.force), custom_call_target="tpu_custom_call" | custom-call | tf_op jit(solution)/shard_map/hand/pallas_call | solution.py:580

commit v6 on v5

--- a/solution.py
+++ b/solution.py
@@ -279,11 +279,14 @@
         return jnp.broadcast_to(far[at, 3, k : k + 1], (ROWS, slots))
 
     def columns(count, where, body):
+        several = next(n for n in (4, 2, 1) if count % n == 0)
+
         def step(i, carry):
-            body(*where(i))
+            for j in range(several):
+                body(*where(i * several + j))
             return carry
 
-        lax.fori_loop(0, count, step, 0)
+        lax.fori_loop(0, count // several, step, 0)
 
     def inner_columns(body):
         columns(sx * sy, lambda i: (i // sy + 1, i % sy + 1), lambda x, y: body(x, y, 1, sz))
@@ -346,15 +349,11 @@
     def middle_cells(body):
         span = sz - 2
         if span > 0:
-            batched(sx * sy * span, 2, lambda i: i // span * sz + 1 + i % span, body, (0,))
+            batched(sx * sy * span, 4, lambda i: i // span * sz + 1 + i % span, body, (0,))
 
     def end_cells(body):
         ends = min(sz, 2)
-        columns(
-            ends * sx * sy,
-            lambda i: (i // ends * sz + i % ends * (sz - 1),),
-            lambda c: body(c, (0,)),
-        )
+        batched(ends * sx * sy, 4, lambda i: i // ends * sz + i % ends * (sz - 1), body, (0,))
 
     def density(c, phases):
         def one_group(g, inside):
@@ -501,9 +500,10 @@
     all_cells(force, 1)
     land_gain(2)
     face_columns(prepare_gain)
+    all_cells(force, 2)
     land_gain(3)
     edge_columns(prepare_gain)
-    last_cells(force, 2, 3)
+    last_cells(force, 3)
 
     scale = FORCE_SCALE * 4.0 * PAIR_SCALE
     pushes = unsort(sorted_rows(3))

time: 23.8 us -> 23.6 us (level)
  no operation moved by 1% of the time
where the time goes in v6:
time: 23.6 us; the launch traced here: 23.4 us
  Pallas kernels  22.8 us (97%)
  between operations  0.64 us (3%)
    pallas_call x1, Pallas kernels, per_device(): pl.pallas_call(functools.partial(kernel, mesh_counts), out_shape=(jax.Sha...  22.1 us
    pallas_call x1, Pallas kernels, per_device(): pl.pallas_call(hand_over, out_shape=tuple((jax.ShapeDtypeStruct(x.shape,...  0.63 us

profile of v6, /device:TPU:0, one launch (start us, length us, event | category | flops | bytes accessed | tf_op | source)
XLA Modules:
  0.0 23.4 jit_solution(8420715754021225662)
XLA Ops:
  0.6 22.1 %atoms.1 = (f32[1,2,8,128]{3,2,1,0:T(8,128)S(1)}, f32[3,1,2,8,128]{4,3,2,1,0:T(8,128)S(1)}) custom-call(s32[1,2,8]{2,1,0:T(2,128)} %counts.1, f32[3,1,2,8,128]{4,3,2,1,0:T(8,128)} %positions.1), custom_call_target="tpu_custom_call" | custom-call | tf_op jit(solution)/shard_map/atoms/pallas_call | solution.py:557
  22.8 0.6 %hand.1 = (f32[1,2,8,128]{3,2,1,0:T(8,128)}, f32[3,1,2,8,128]{4,3,2,1,0:T(8,128)}) custom-call(f32[1,2,8,128]{3,2,1,0:T(8,128)S(1)} %get-tuple-element.4.energy, f32[3,1,2,8,128]{4,3,2,1,0:T(8,128)S(1)} %get-tuple-element.5.force), custom_call_target="tpu_custom_call" | custom-call | tf_op jit(solution)/shard_map/hand/pallas_call | solution.py:580

commit v7 on v6

--- a/solution.py
+++ b/solution.py
@@ -318,9 +318,9 @@
 
     slot_lane = lax.broadcasted_iota(jnp.int32, (ROWS, slots), 1)
 
-    def lane_sums(c, rows, parts):
+    def lane_sums(c, rows, parts, kind=0):
         kept = dense[rows, :]
-        for k, part in enumerate(parts):
+        for k, part in enumerate(parts, kind):
             kept = jnp.where(
                 slot_lane == k * cells + c, jnp.sum(part, axis=1, keepdims=True), kept
             )
@@ -358,10 +358,11 @@
     def density(c, phases):
         def one_group(g, inside):
             xi, yi, zi, ci = (lanes_of[held_at(c, g, k)] for k in range(4))
-            if phases[0]:
-                rho, quartic = lanes_of[held_at(c, g, 4)], lanes_of[held_at(c, g, 5)]
+            early = phases[0] == 0
+            if early:
+                rho, quartic = (jnp.zeros((ROWS, slots), jnp.float32),) * 2
             else:
-                rho, quartic = (jnp.zeros((ROWS, slots), jnp.float32),) * 2
+                rho = lanes_of[held_at(c, g, 4)]
             for phase in phases:
                 base = table[c, phase * SPAN + g]
                 for step in range(2):
@@ -372,12 +373,26 @@
                     weights[held_at(c, g, 2 * phase + step)] = w
                     s = w * w
                     rho = rho + s
-                    quartic = quartic + s * s
+                    if early:
+                        quartic = quartic + s * s
             if phases[-1] == 3:
-                lane_sums(c, pl.ds(g * ROWS, ROWS), (rho, quartic))
+                lane_sums(c, pl.ds(g * ROWS, ROWS), (rho,))
             else:
                 lanes_of[held_at(c, g, 4)] = rho
+            if early:
                 lanes_of[held_at(c, g, 5)] = quartic
+            return inside
+
+        lax.fori_loop(0, group_count, one_group, 0, unroll=True)
+
+    def quartics(c, phases):
+        def one_group(g, inside):
+            quartic = lanes_of[held_at(c, g, 5)]
+            for i in range(2, 8):
+                w = weights[held_at(c, g, i)]
+                s = w * w
+                quartic = quartic + s * s
+            lane_sums(c, pl.ds(g * ROWS, ROWS), (quartic,), 1)
             return inside
 
         lax.fori_loop(0, group_count, one_group, 0, unroll=True)
@@ -457,20 +472,14 @@
     edge_columns(prepare)
     last_cells(density, 3)
 
-    rho_rows, quartic_rows = sorted_rows(2)
+    rho_rows = sorted_rows(1)[0]
     first = jnp.maximum(rho_rows - 1.0, 0.0)
-    second = jnp.maximum(quartic_rows - 1.0, 0.0)
     fprime = -0.5 * EMBED_SCALE * lax.rsqrt(first + 1.0)
     gain = 0.5 - fprime * (0.5 / PAIR_SCALE)
     gain_rows = unsort([gain])[0]
     gain_own[...] = gain_rows.reshape(sizes + (1, slots))
     send_rims(mesh_counts, gain_own, gain_ext, sent, gain_landed)
     gain_ext[inner] = gain_rows.reshape(sizes + (1, slots))
-    pair_sum = PAIR_SCALE * (second - 2.0 * first)
-    energy = -EMBED_SCALE * jnp.sqrt(first + 1.0) + 0.5 * pair_sum
-    energy_rows = unsort([energy])[0]
-    energy_ref[...] = jnp.where(filled, energy_rows, 0.0).reshape(sizes + (slots,))
-
     tall = [piece.astype(jnp.float32) for piece in halves(gain)]
     tall += [jnp.zeros((slots - 2 * cells, depth), jnp.float32)]
     tall = jnp.concatenate(tall, axis=0)
@@ -489,6 +498,13 @@
                 lanes_of[held_at(pair * i + j, g, 3)] = spread[
                     g * ROWS : (g + 1) * ROWS, j * slots : (j + 1) * slots
                 ]
+
+    last_cells(quartics)
+    second = jnp.maximum(sorted_rows(2)[1] - 1.0, 0.0)
+    pair_sum = PAIR_SCALE * (second - 2.0 * first)
+    energy = -EMBED_SCALE * jnp.sqrt(first + 1.0) + 0.5 * pair_sum
+    energy_rows = unsort([energy])[0]
+    energy_ref[...] = jnp.where(filled, energy_rows, 0.0).reshape(sizes + (slots,))
 
     inner_columns(prepare_gain)
     middle_cells(force)

time: 23.6 us -> 22.9 us (0.970)
  Pallas kernels: 22.8 us -> 21.9 us
    pallas_call x1, Pallas kernels: 22.1 us -> 21.3 us  [per_device(): pl.pallas_call(functools.partial(kernel, mesh_counts), out_shape=(jax.Sha...]
where the time goes in v7:
time: 22.9 us; the launch traced here: 22.6 us
  Pallas kernels  21.9 us (96%)
  between operations  0.64 us (3%)
    pallas_call x1, Pallas kernels, per_device(): pl.pallas_call(functools.partial(kernel, mesh_counts), out_shape=(jax.Sha...  21.3 us
    pallas_call x1, Pallas kernels, per_device(): pl.pallas_call(hand_over, out_shape=tuple((jax.ShapeDtypeStruct(x.shape,...  0.63 us

profile of v7, /device:TPU:0, one launch (start us, length us, event | category | flops | bytes accessed | tf_op | source)
XLA Modules:
  0.0 22.6 jit_solution(935937374064964885)
XLA Ops:
  0.6 21.3 %atoms.1 = (f32[1,2,8,128]{3,2,1,0:T(8,128)S(1)}, f32[3,1,2,8,128]{4,3,2,1,0:T(8,128)S(1)}) custom-call(s32[1,2,8]{2,1,0:T(2,128)} %counts.1, f32[3,1,2,8,128]{4,3,2,1,0:T(8,128)} %positions.1), custom_call_target="tpu_custom_call" | custom-call | tf_op jit(solution)/shard_map/atoms/pallas_call | solution.py:573
  21.9 0.6 %hand.1 = (f32[1,2,8,128]{3,2,1,0:T(8,128)}, f32[3,1,2,8,128]{4,3,2,1,0:T(8,128)}) custom-call(f32[1,2,8,128]{3,2,1,0:T(8,128)S(1)} %get-tuple-element.4.energy, f32[3,1,2,8,128]{4,3,2,1,0:T(8,128)S(1)} %get-tuple-element.5.force), custom_call_target="tpu_custom_call" | custom-call | tf_op jit(solution)/shard_map/hand/pallas_call | solution.py:596

commit v8 on v7

--- a/solution.py
+++ b/solution.py
@@ -392,7 +392,7 @@
                 w = weights[held_at(c, g, i)]
                 s = w * w
                 quartic = quartic + s * s
-            lane_sums(c, pl.ds(g * ROWS, ROWS), (quartic,), 1)
+            lane_sums(c, pl.ds(g * ROWS, ROWS), (quartic,), 3)
             return inside
 
         lax.fori_loop(0, group_count, one_group, 0, unroll=True)
@@ -500,12 +500,6 @@
                 ]
 
     last_cells(quartics)
-    second = jnp.maximum(sorted_rows(2)[1] - 1.0, 0.0)
-    pair_sum = PAIR_SCALE * (second - 2.0 * first)
-    energy = -EMBED_SCALE * jnp.sqrt(first + 1.0) + 0.5 * pair_sum
-    energy_rows = unsort([energy])[0]
-    energy_ref[...] = jnp.where(filled, energy_rows, 0.0).reshape(sizes + (slots,))
-
     inner_columns(prepare_gain)
     middle_cells(force)
     land_gain(0)
@@ -522,7 +516,12 @@
     last_cells(force, 3)
 
     scale = FORCE_SCALE * 4.0 * PAIR_SCALE
-    pushes = unsort(sorted_rows(3))
+    *pushes, quartic_rows = sorted_rows(4)
+    second = jnp.maximum(quartic_rows - 1.0, 0.0)
+    pair_sum = PAIR_SCALE * (second - 2.0 * first)
+    energy = -EMBED_SCALE * jnp.sqrt(first + 1.0) + 0.5 * pair_sum
+    *pushes, energy_rows = unsort(pushes + [energy])
+    energy_ref[...] = jnp.where(filled, energy_rows, 0.0).reshape(sizes + (slots,))
     for k, push in enumerate(pushes):
         force_ref[k] = jnp.where(filled, scale * push, 0.0).reshape(sizes + (slots,))
 
@@ -566,7 +565,7 @@
         ((cells, groups, quads, 4, ROWS, slots), f32),
         ((cells, groups, quads, 4, ROWS, slots), f32),
         ((-(-depth // 128) * 128, slots), f32),
-        ((2, 6 * cells, 2 * slots), f32),
+        ((2, 8 * cells, 2 * slots), f32),
         ((cells, slots), i32),
     ]
     held = sum(math.prod(shape) * jnp.dtype(kind).itemsize for shape, kind in vmem)

time: 22.9 us -> 22.9 us (level)
  no operation moved by 1% of the time
where the time goes in v8:
time: 22.9 us; the launch traced here: 22.6 us
  Pallas kernels  22 us (96%)
  between operations  0.64 us (3%)
    pallas_call x1, Pallas kernels, per_device(): pl.pallas_call(functools.partial(kernel, mesh_counts), out_shape=(jax.Sha...  21.3 us
    pallas_call x1, Pallas kernels, per_device(): pl.pallas_call(hand_over, out_shape=tuple((jax.ShapeDtypeStruct(x.shape,...  0.63 us

profile of v8, /device:TPU:0, one launch (start us, length us, event | category | flops | bytes accessed | tf_op | source)
XLA Modules:
  0.0 22.6 jit_solution(16606354688679395583)
XLA Ops:
  0.6 21.3 %atoms.1 = (f32[1,2,8,128]{3,2,1,0:T(8,128)S(1)}, f32[3,1,2,8,128]{4,3,2,1,0:T(8,128)S(1)}) custom-call(s32[1,2,8]{2,1,0:T(2,128)} %counts.1, f32[3,1,2,8,128]{4,3,2,1,0:T(8,128)} %positions.1), custom_call_target="tpu_custom_call" | custom-call | tf_op jit(solution)/shard_map/atoms/pallas_call | solution.py:572
  22.0 0.6 %hand.1 = (f32[1,2,8,128]{3,2,1,0:T(8,128)}, f32[3,1,2,8,128]{4,3,2,1,0:T(8,128)}) custom-call(f32[1,2,8,128]{3,2,1,0:T(8,128)S(1)} %get-tuple-element.4.energy, f32[3,1,2,8,128]{4,3,2,1,0:T(8,128)S(1)} %get-tuple-element.5.force), custom_call_target="tpu_custom_call" | custom-call | tf_op jit(solution)/shard_map/hand/pallas_call | solution.py:595
